TPU v7x, 32 devices: a whole 2x2x4 slice. The times are simulated.
32 devices in a mesh: ctx: 8 (over z, x), dp: 4 (over y, core).
Axes of the slice: x: 2, y: 2, z: 4, core: 2. Of those that a mesh axis runs over, the one named last changes fastest.
Arguments:
- head_input: bfloat16 [8192, 4096], P(('dp', 'ctx')), parts along dimension 0, may hold values from -6 to 6
- gate_input: bfloat16 [8192, 4096], P(('dp', 'ctx')), parts along dimension 0, may hold values from -6 to 6
- write_vector: bfloat16 [8192, 128], P(('dp', 'ctx')), parts along dimension 0, may hold values from -2.5 to 2.5
- read_vector: bfloat16 [8192, 128], P(('dp', 'ctx')), parts along dimension 0, may hold values from -2.5 to 2.5
- increment_preactivation: bfloat16 [8192, 64], P(('dp', 'ctx')), parts along dimension 0, may hold values from -2 to 8
- step_bias: float32 [64], replicated, may hold values from -1 to 0.5
- decay_log: float32 [64], replicated, may hold values from -9.3 to -2.3
- skip_gain: float32 [64], replicated, may hold values from 0.5 to 1.5
- norm_weight: float32 [4096], replicated, may hold values from 0.5 to 1.5
- doc_starts: int32 [64], P(('dp', 'ctx')), parts along dimension 0, may hold values from 0 to 1, as said below
- block_order: int32 [64], P(('dp', 'ctx')), parts along dimension 0, may hold values from 0 to 15, as said below
Outputs:
- packed_out: bfloat16 [8192, 4096], P(('dp', 'ctx')), parts along dimension 0
There are 4 independent parts, one for each index of `dp`. A program takes and returns all parts, laid end to end along the dimension named above; an argument that names none is the same for every part. Nothing has to cross between parts.
Inputs may be any that keep to these rules, and one draw needn't show every extreme that they name: `doc_starts`: block 0 starts a document; no document is longer than 128 blocks. `block_order`: a permutation of the block indices that keeps each document's blocks together and in their order.
All inputs are finite; a program needn't handle non-finite values.
Results may differ from a plain program's by a relative error of at most 0.0085.
Values may be sent and summed in bfloat16 or wider, within the bound.
A program may use at most 128 MiB of HBM per device.

v0:
```python
import functools

import jax
import jax.numpy as jnp
from jax import lax
from jax.experimental import pallas as pl
from jax.experimental.pallas import tpu as pltpu
from jax.sharding import PartitionSpec as P

HEAD_DIM = 64
GROUP = 128
CHUNK = 8
WIDE = CHUNK * HEAD_DIM
EXTRA = 16

highest = lax.Precision.HIGHEST
VM = pl.BlockSpec(memory_space=pltpu.VMEM)
SM = pl.BlockSpec(memory_space=pltpu.SMEM)


def transposed(v):
    rows, cols = v.shape
    if cols < 128:
        v = jnp.concatenate([v, jnp.zeros((rows, 128 - cols), v.dtype)], axis=1)
    return v.T[:cols]


def lower_mask():
    row = lax.broadcasted_iota(jnp.int32, (GROUP, GROUP), 0)
    col = lax.broadcasted_iota(jnp.int32, (GROUP, GROUP), 1)
    return row >= col


def step_terms(logit_ref, bias_ref, dlog_ref):
    v = logit_ref[...].astype(jnp.float32) + bias_ref[...]
    dt = jnp.maximum(v, 0.0) + jnp.log(1.0 + jnp.exp(-jnp.abs(v)))
    return dt, -dt * jnp.exp(dlog_ref[...])


def spread(v):
    rows = v.shape[0]
    first = lax.broadcasted_iota(jnp.int32, (rows, 128), 1) < HEAD_DIM
    return jnp.concatenate(
        [
            jnp.where(first, v[:, k : k + 1], v[:, k + 1 : k + 2])
            for k in range(0, CHUNK, 2)
        ],
        axis=1,
    )


def prepare(logit_ref, bias_ref, dlog_ref, write_ref, cum_s, dt_s, write_t):
    heads = bias_ref.shape[1]
    dt, fall = step_terms(logit_ref, bias_ref, dlog_ref)
    tri = lower_mask().astype(jnp.float32)
    cums = []
    for g in range(write_t.shape[0]):
        rows = slice(g * GROUP, (g + 1) * GROUP)
        cum = jnp.dot(tri, fall[rows], precision=highest, preferred_element_type=jnp.float32)
        cums.append(cum)
        for c in range(heads // CHUNK):
            cum_s[g, c] = cum[:, c * CHUNK : (c + 1) * CHUNK]
            dt_s[g, c] = dt[rows, c * CHUNK : (c + 1) * CHUNK]
        write_t[g] = write_ref[rows, :].astype(jnp.float32).T.astype(jnp.bfloat16)
    return dt, cums


def group_state(g, c, x, cum_s, dt_s, write_t):
    cum = cum_s[g, c]
    last = cum[GROUP - 1 : GROUP]
    tail = jnp.exp(last - cum) * dt_s[g, c]
    scaled = (x.astype(jnp.float32) * spread(tail)).astype(jnp.bfloat16)
    state = jnp.dot(write_t[g], scaled, preferred_element_type=jnp.float32)
    return state, spread(jnp.exp(last))


def state_kernel(
    x_ref, logit_ref, write_ref, bias_ref, dlog_ref, starts_ref, order_ref, out_ref, cum_s, dt_s, write_t
):
    groups = write_t.shape[0]
    prepare(logit_ref, bias_ref, dlog_ref, write_ref, cum_s, dt_s, write_t)
    parts, _, width = out_ref.shape
    chunks = cum_s.shape[1]
    per = width // WIDE

    def one(c, carry):
        cols = pl.ds(pl.multiple_of(c * WIDE, WIDE), WIDE)
        total, decay = None, None
        for g in range(groups):
            x = x_ref[g * GROUP : (g + 1) * GROUP, cols]
            state, last = group_state(g, c, x, cum_s, dt_s, write_t)
            keep = 1.0 - starts_ref[g].astype(jnp.float32)
            factor = keep * last
            total = state if total is None else factor * total + state
            decay = factor if decay is None else factor * decay
        coarse = decay.astype(jnp.bfloat16)
        fine = (decay - coarse.astype(jnp.float32)).astype(jnp.bfloat16)
        row = lax.broadcasted_iota(jnp.int32, (EXTRA, WIDE), 0)
        lane = lax.broadcasted_iota(jnp.int32, (EXTRA, WIDE), 1)
        order = jnp.zeros((EXTRA, WIDE), jnp.float32)
        for g in range(groups):
            order = jnp.where(lane == g, order_ref[g].astype(jnp.float32), order)
        extra = jnp.where(
            row == 0,
            coarse.astype(jnp.float32),
            jnp.where(row == 1, fine.astype(jnp.float32), order),
        )
        full = jnp.concatenate([total, extra], axis=0).astype(jnp.bfloat16)
        if parts == 1:
            out_ref[0, :, cols] = full
        else:
            into = pl.ds(pl.multiple_of((c % per) * WIDE, WIDE), WIDE)
            out_ref[c // per, :, into] = full
        return carry

    lax.fori_loop(0, chunks, one, 0)


def scan_kernel(in_ref, out_ref):
    parts, _, width = in_ref.shape
    state = jnp.zeros((GROUP, width), jnp.float32)
    for s in range(parts):
        out_ref[s] = state.astype(jnp.bfloat16)
        extra = in_ref[s, GROUP : GROUP + EXTRA, :].astype(jnp.float32)
        decay = extra[0:1] + extra[1:2]
        state = decay * state + in_ref[s, :GROUP, :].astype(jnp.float32)


def gated_setup(
    logit_ref, bias_ref, dlog_ref, write_ref, read_ref, gain_ref, cum_s, dt_s, write_t, cum_t, dt_t, gain_s, score_s
):
    groups, chunks = cum_s.shape[:2]
    dt, cums = prepare(logit_ref, bias_ref, dlog_ref, write_ref, cum_s, dt_s, write_t)
    mask = lower_mask()
    for g in range(groups):
        rows = slice(g * GROUP, (g + 1) * GROUP)
        ct = transposed(cums[g])
        dtt = transposed(dt[rows])
        for c in range(chunks):
            cum_t[g, c] = ct[c * CHUNK : (c + 1) * CHUNK]
            dt_t[g, c] = dtt[c * CHUNK : (c + 1) * CHUNK]
        score = jnp.dot(read_ref[rows, :], write_t[g], preferred_element_type=jnp.float32)
        score_s[g] = jnp.where(mask, score, 0.0)
    for c in range(chunks):
        gain_s[c] = jnp.broadcast_to(gain_ref[:, c * CHUNK : (c + 1) * CHUNK], (8, CHUNK))


def gated_chunk(
    c, state, put, x_ref, gate_ref, read_ref, starts_ref, cum_s, dt_s, write_t, cum_t, dt_t, gain_s, score_s
):
    groups = cum_s.shape[0]
    first = lax.broadcasted_iota(jnp.int32, (GROUP, 128), 1) < HEAD_DIM
    cols = pl.ds(pl.multiple_of(c * WIDE, WIDE), WIDE)
    gain = spread(gain_s[c][0:1])
    for g in range(groups):
        rows = slice(g * GROUP, (g + 1) * GROUP)
        x = x_ref[rows, cols]
        keep = 1.0 - starts_ref[g].astype(jnp.float32)
        entering = (keep * state).astype(jnp.bfloat16)
        cum = cum_s[g, c]
        carried = jnp.dot(read_ref[rows, :], entering, preferred_element_type=jnp.float32)
        mixed = carried * spread(jnp.exp(cum)) + gain * x.astype(jnp.float32)
        score = score_s[g]
        ct, dtt = cum_t[g, c], dt_t[g, c]
        pieces = []
        for k in range(0, CHUNK, 2):
            pair = x[:, k * HEAD_DIM : (k + 2) * HEAD_DIM]
            both = []
            for h in (k, k + 1):
                gap = cum[:, h : h + 1] - ct[h : h + 1]
                weight = score * jnp.exp(jnp.minimum(gap, 0.0)) * dtt[h : h + 1]
                both.append(
                    jnp.dot(weight.astype(jnp.bfloat16), pair, preferred_element_type=jnp.float32)
                )
            pieces.append(jnp.where(first, both[0], both[1]))
        mixed = mixed + jnp.concatenate(pieces, axis=1)
        gate = gate_ref[rows, cols].astype(jnp.float32)
        put(g, (mixed * (gate / (1.0 + jnp.exp(-gate)))).astype(jnp.bfloat16))
        if g + 1 < groups:
            own, last = group_state(g, c, x, cum_s, dt_s, write_t)
            state = keep * last * state + own


def gated_kernel(
    x_ref,
    gate_ref,
    logit_ref,
    write_ref,
    read_ref,
    entry_ref,
    bias_ref,
    dlog_ref,
    gain_ref,
    starts_ref,
    out_ref,
    *scratch,
):
    gated_setup(logit_ref, bias_ref, dlog_ref, write_ref, read_ref, gain_ref, *scratch)
    parts, _, width = out_ref.shape
    chunks = scratch[0].shape[1]
    per = width // WIDE

    def one(c, carry):
        cols = pl.ds(pl.multiple_of(c * WIDE, WIDE), WIDE)
        into = pl.ds(pl.multiple_of((c % per) * WIDE, WIDE), WIDE)
        if parts == 1:
            state = entry_ref[0, :, cols].astype(jnp.float32)
        else:
            state = entry_ref[c // per, :, into].astype(jnp.float32)

        def put(g, value):
            rows = slice(g * GROUP, (g + 1) * GROUP)
            if parts == 1:
                out_ref[0, rows, cols] = value
            else:
                out_ref[c // per, rows, into] = value

        gated_chunk(c, state, put, x_ref, gate_ref, read_ref, starts_ref, *scratch)
        return carry

    lax.fori_loop(0, chunks, one, 0)


def fused_kernel(
    n,
    x_ref,
    gate_ref,
    logit_ref,
    write_ref,
    read_ref,
    bias_ref,
    dlog_ref,
    gain_ref,
    weight_ref,
    starts_ref,
    order_ref,
    out_ref,
    fin,
    fout,
    total_s,
    decay_s,
    made,
    got,
    stage,
    final,
    chain_send,
    chain_recv,
    send1,
    recv1,
    send2,
    recv2,
    send3,
    recv3,
    order_all,
    order_s,
    order_sem,
    *scratch,
):
    cum_s, dt_s, write_t = scratch[:3]
    groups = cum_s.shape[0]
    me = lax.axis_index("ctx")
    offsets = range(1, n)
    half = n // 2
    mine = (me // half) * half
    other = half - mine

    def partner(k):
        far = 1 - k % 2
        return far * other + (1 - far) * mine + lax.rem(me + k // 2, half)

    barrier = pltpu.get_barrier_semaphore()
    for off in range(1, n):
        pl.semaphore_signal(
            barrier, inc=1, device_id={"ctx": lax.rem(me + off, n)}, device_id_type=pl.DeviceIdType.MESH
        )
    gated_setup(logit_ref, bias_ref, dlog_ref, write_ref, read_ref, gain_ref, *scratch)

    @pl.when(me == 0)
    def _():
        fin[...] = jnp.zeros_like(fin)

    def chain(c):
        return pltpu.make_async_remote_copy(
            src_ref=fout.at[c],
            dst_ref=fin.at[c],
            send_sem=chain_send.at[c],
            recv_sem=chain_recv.at[c],
            device_id={"ctx": lax.rem(me + 1, n)},
            device_id_type=pl.DeviceIdType.MESH,
        )

    def spread_order(there, slot):
        return pltpu.make_async_remote_copy(
            src_ref=order_ref,
            dst_ref=order_all.at[slot],
            send_sem=send3.at[there],
            recv_sem=recv3.at[slot],
            device_id={"ctx": there},
            device_id_type=pl.DeviceIdType.MESH,
        )

    def outward(source, target, sends, recvs, there, slot):
        return pltpu.make_async_remote_copy(
            src_ref=source.at[there],
            dst_ref=target.at[pl.ds(slot * groups, groups)] if target is got else target.at[slot],
            send_sem=sends.at[there],
            recv_sem=recvs.at[slot],
            device_id={"ctx": there},
            device_id_type=pl.DeviceIdType.MESH,
        )

    pl.semaphore_wait(barrier, n - 1)
    order_all[me] = order_ref[...]
    for off in offsets:
        spread_order(lax.rem(me + off, n), me).start()

    def ends(c, carry):
        cols = pl.ds(pl.multiple_of(c * WIDE, WIDE), WIDE)
        total, decay = None, None
        for g in range(groups):
            x = x_ref[g * GROUP : (g + 1) * GROUP, cols]
            state, last = group_state(g, c, x, cum_s, dt_s, write_t)
            factor = (1.0 - starts_ref[g].astype(jnp.float32)) * last
            total = state if total is None else factor * total + state
            decay = factor if decay is None else factor * decay
        total_s[c] = total
        decay_s[c] = jnp.broadcast_to(decay, (8, WIDE))

        @pl.when(me == 0)
        def _():
            fout[c] = total.astype(jnp.bfloat16)
            chain(c).start()

        return carry

    lax.fori_loop(0, n, ends, 0)

    def relay(c, carry):
        chain(c).wait_recv()

        @pl.when(me < n - 1)
        def _():
            state = fin[c].astype(jnp.float32)
            fout[c] = (decay_s[c][0:1] * state + total_s[c]).astype(jnp.bfloat16)
            chain(c).start()

        return carry

    @pl.when(me > 0)
    def _():
        lax.fori_loop(0, n, relay, 0)

    def one(k, carry):
        c = partner(k)
        state = fin[c].astype(jnp.float32)

        def put(g, value):
            made[c, g] = value

        gated_chunk(c, state, put, x_ref, gate_ref, read_ref, starts_ref, *scratch)

        @pl.when(c != me)
        def _():
            outward(made, got, send1, recv1, c, me).start()

        @pl.when(c == me)
        def _():
            for g in range(groups):
                got[me * groups + g] = made[c, g]

        return carry

    lax.fori_loop(0, n, one, 0)
    for off in offsets:
        there = lax.rem(me + off, n)
        spread_order(there, there).wait_recv()
    fetch = pltpu.make_async_copy(order_all, order_s, order_sem)
    fetch.start()
    fetch.wait()
    for off in offsets:
        there = lax.rem(me + off, n)
        outward(made, got, send1, recv1, there, there).wait_recv()

    def second(k, carry):
        there = partner(k)
        for g in range(groups):
            stage[there, g] = got[order_s[there, 0, g]]

        @pl.when(there != me)
        def _():
            outward(stage, final, send2, recv2, there, me).start()

        return carry

    lax.fori_loop(0, n, second, 0)
    for g in range(groups):
        final[me, g] = stage[me, g]

    @pl.when(me < n - 1)
    def _():
        for c in range(n):
            chain(c).wait_send()

    for off in offsets:
        there = lax.rem(me + off, n)
        outward(made, got, send1, recv1, there, there).wait_send()
        outward(stage, final, send2, recv2, there, there).wait_send()
        spread_order(there, there).wait_send()
    for off in offsets:
        there = lax.rem(me + off, n)
        outward(stage, final, send2, recv2, there, there).wait_recv()
    tile = 32
    for g in range(groups):

        def norm(r, carry):
            at = pl.ds(pl.multiple_of(r * tile, tile), tile)
            total = jnp.zeros((tile, 1), jnp.float32)
            for s in range(n):
                v = final[s, g, at, :].astype(jnp.float32)
                total = total + jnp.sum(v * v, axis=1, keepdims=True)
            scale = lax.rsqrt(total * (1.0 / (n * WIDE)) + 1e-05)
            for s in range(n):
                v = final[s, g, at, :].astype(jnp.float32)
                w = weight_ref[:, s * WIDE : (s + 1) * WIDE]
                into = pl.ds(pl.multiple_of(g * GROUP + r * tile, tile), tile)
                out_ref[into, s * WIDE : (s + 1) * WIDE] = (v * scale * w).astype(jnp.bfloat16)
            return carry

        lax.fori_loop(0, GROUP // tile, norm, 0)


def norm_kernel(in_ref, weight_ref, out_ref):
    parts, rows, width = in_ref.shape
    tile = 32

    def one(r, carry):
        at = pl.ds(pl.multiple_of(r * tile, tile), tile)
        total = jnp.zeros((tile, 1), jnp.float32)
        for s in range(parts):
            v = in_ref[s, at, :].astype(jnp.float32)
            total = total + jnp.sum(v * v, axis=1, keepdims=True)
        scale = lax.rsqrt(total * (1.0 / (parts * width)) + 1e-05)
        for s in range(parts):
            v = in_ref[s, at, :].astype(jnp.float32)
            w = weight_ref[:, s * width : (s + 1) * width]
            out_ref[at, s * width : (s + 1) * width] = (v * scale * w).astype(jnp.bfloat16)
        return carry

    lax.fori_loop(0, rows // tile, one, 0)


def local(
    head_input,
    gate_input,
    write_vector,
    read_vector,
    increment_preactivation,
    step_bias,
    decay_log,
    skip_gain,
    norm_weight,
    doc_starts,
    block_order,
):
    devices = lax.axis_size("ctx")
    rows, features = head_input.shape
    heads = step_bias.shape[0]
    groups = rows // GROUP
    chunks = heads // CHUNK
    width = features // devices
    state_size = write_vector.shape[1]
    direct = width % WIDE == 0
    parts = devices if direct else 1
    limit = pltpu.CompilerParams(vmem_limit_bytes=48 * 1024 * 1024)
    common = [
        pltpu.VMEM((groups, chunks, GROUP, CHUNK), jnp.float32),
        pltpu.VMEM((groups, chunks, GROUP, CHUNK), jnp.float32),
        pltpu.VMEM((groups, state_size, GROUP), jnp.bfloat16),
    ]
    more = [
        pltpu.VMEM((groups, chunks, CHUNK, GROUP), jnp.float32),
        pltpu.VMEM((groups, chunks, CHUNK, GROUP), jnp.float32),
        pltpu.VMEM((chunks, 8, CHUNK), jnp.float32),
        pltpu.VMEM((groups, GROUP, GROUP), jnp.float32),
    ]
    bias, dlog, gain = (v.reshape(1, -1) for v in (step_bias, decay_log, skip_gain))

    def to_owners(v):
        if not direct:
            v = v.reshape(v.shape[1], devices, width).transpose(1, 0, 2)
        return lax.all_to_all(v, "ctx", split_axis=0, concat_axis=0, tiled=True)

    def joined(v):
        if not direct:
            v = v.transpose(1, 0, 2).reshape(1, v.shape[1], features)
        return v

    if width == WIDE and devices % 2 == 0:
        order = jnp.broadcast_to(jnp.pad(block_order, (0, 128 - groups))[None], (8, 128))
        slab = (devices, groups, GROUP, WIDE)
        return pl.pallas_call(
            functools.partial(fused_kernel, devices),
            out_shape=jax.ShapeDtypeStruct((rows, features), jnp.bfloat16),
            in_specs=[VM] * 9 + [SM, VM],
            out_specs=VM,
            scratch_shapes=[
                pltpu.VMEM((devices, state_size, WIDE), jnp.bfloat16),
                pltpu.VMEM((devices, state_size, WIDE), jnp.bfloat16),
                pltpu.VMEM((devices, state_size, WIDE), jnp.float32),
                pltpu.VMEM((devices, 8, WIDE), jnp.float32),
                pltpu.VMEM(slab, jnp.bfloat16),
                pltpu.VMEM((devices * groups, GROUP, WIDE), jnp.bfloat16),
                pltpu.VMEM(slab, jnp.bfloat16),
                pltpu.VMEM(slab, jnp.bfloat16),
            ]
            + [pltpu.SemaphoreType.DMA((devices,))] * 8
            + [
                pltpu.VMEM((devices, 8, 128), jnp.int32),
                pltpu.SMEM((devices, 8, 128), jnp.int32),
                pltpu.SemaphoreType.DMA,
            ]
            + common
            + more,
            compiler_params=pltpu.CompilerParams(
                collective_id=0, has_side_effects=True, vmem_limit_bytes=56 * 1024 * 1024
            ),
            name="fused",
        )(
            head_input,
            gate_input,
            increment_preactivation,
            write_vector,
            read_vector,
            bias,
            dlog,
            gain,
            norm_weight.reshape(1, -1),
            doc_starts,
            order,
        )

    ends = pl.pallas_call(
        state_kernel,
        out_shape=jax.ShapeDtypeStruct((parts, state_size + EXTRA, features // parts), jnp.bfloat16),
        in_specs=[VM] * 5 + [SM] * 2,
        out_specs=VM,
        scratch_shapes=common,
        compiler_params=limit,
        name="end_states",
    )(head_input, increment_preactivation, write_vector, bias, dlog, doc_starts, block_order)
    ends = to_owners(ends)
    all_order = ends[:, state_size + 2, :groups].astype(jnp.int32).reshape(-1)
    entry = pl.pallas_call(
        scan_kernel,
        out_shape=jax.ShapeDtypeStruct((devices, state_size, width), jnp.bfloat16),
        in_specs=[VM],
        out_specs=VM,
        compiler_params=limit,
        name="scan_states",
    )(ends)
    entry = joined(lax.all_to_all(entry, "ctx", split_axis=0, concat_axis=0, tiled=True))
    gated = pl.pallas_call(
        gated_kernel,
        out_shape=jax.ShapeDtypeStruct((parts, rows, features // parts), jnp.bfloat16),
        in_specs=[VM] * 9 + [SM],
        out_specs=VM,
        scratch_shapes=common
        + more,
        compiler_params=limit,
        name="gated",
    )(
        head_input,
        gate_input,
        increment_preactivation,
        write_vector,
        read_vector,
        entry,
        bias,
        dlog,
        gain,
        doc_starts,
    )
    gated = to_owners(gated)
    blocks = gated.reshape(devices * groups, GROUP, width)[all_order]
    packed = lax.all_to_all(
        blocks.reshape(devices, rows, width), "ctx", split_axis=0, concat_axis=0, tiled=True
    )
    return pl.pallas_call(
        norm_kernel,
        out_shape=jax.ShapeDtypeStruct((rows, features), jnp.bfloat16),
        in_specs=[VM] * 2,
        out_specs=VM,
        compiler_params=limit,
        name="norm",
    )(joined(packed), norm_weight.reshape(1, -1))


def solution(mesh):
    return jax.shard_map(
        local,
        mesh=mesh,
        in_specs=(
            P(("dp", "ctx"), None),
            P(("dp", "ctx"), None),
            P(("dp", "ctx"), None),
            P(("dp", "ctx"), None),
            P(("dp", "ctx"), None),
            P(),
            P(),
            P(),
            P(),
            P(("dp", "ctx")),
            P(("dp", "ctx")),
        ),
        out_specs=P(("dp", "ctx"), None),
        check_vma=False,
    )
```

profile of v0, /device:TPU:0, one launch (start us, length us, event | category | flops | bytes accessed | tf_op | source)
XLA Modules:
  0.0 173.0 jit_solution(15754723835029018646)
XLA Ops:
  0.0 0.7 pad.4
  0.7 0.6 broadcast_in_dim.2.order_ref
  1.3 1.5 copy.12.logit_ref
  2.7 167.1 %fused.1 = bf16[256,4096]{1,0:T(8,128)(2,1)} custom-call(bf16[256,4096]{1,0:T(8,128)(2,1)} %x_ref.1, bf16[256,4096]{1,0:T(8,128)(2,1)} %gate_ref.1, bf16[256,64]{1,0:T(8,128)(2,1)} %copy.12.logit_ref, bf16[256,128]{1,0:T(8,128)(2,1)} %write_ref.1, bf16[256,128]{1,0:T(8,128)(2,1)} %read_ref.1, f32[1,64]{1,0:T(1,128)} %bitcast.5, f32[1,64]{1,0:T(1,128)} %bitcast.6, ...), custom_call_target="tpu_custom_call" | custom-call | tf_op jit(solution)/shard_map/fused/pallas_call | solution.py:501
  169.9 3.1 %copy.14 = bf16[256,4096]{1,0:T(8,128)(2,1)} copy(bf16[256,4096]{1,0:T(8,128)(2,1)} %fused.1) | data formatting | bytes 4194304
where the time goes:
time: 173 us
  Pallas kernels  167 us (97%)
  local copies, waits for them, and re-layouts  5.88 us (3%)
    pallas_call x1, Pallas kernels, local(): pl.pallas_call(functools.partial(fused_kernel, devices), out_shape=jax.Sh...  167 us
    unnamed x2, local copies, waits for them, and re-layouts  4.62 us

commit v1 on v0

--- a/solution.py
+++ b/solution.py
@@ -12,10 +12,12 @@
 CHUNK = 8
 WIDE = CHUNK * HEAD_DIM
 EXTRA = 16
+PARTS = 4
 
 highest = lax.Precision.HIGHEST
 VM = pl.BlockSpec(memory_space=pltpu.VMEM)
 SM = pl.BlockSpec(memory_space=pltpu.SMEM)
+ANY = pl.BlockSpec(memory_space=pl.ANY)
 
 
 def transposed(v):
@@ -25,6 +27,13 @@
     return v.T[:cols]
 
 
+def upright(v):
+    rows, cols = v.shape
+    if rows < 128:
+        v = jnp.concatenate([v, jnp.zeros((128 - rows, cols), v.dtype)], axis=0)
+    return v.T[:, :rows]
+
+
 def lower_mask():
     row = lax.broadcasted_iota(jnp.int32, (GROUP, GROUP), 0)
     col = lax.broadcasted_iota(jnp.int32, (GROUP, GROUP), 1)
@@ -32,7 +41,9 @@
 
 
 def step_terms(logit_ref, bias_ref, dlog_ref):
-    v = logit_ref[...].astype(jnp.float32) + bias_ref[...]
+    raw = logit_ref[...].astype(jnp.float32)
+    raw = jnp.concatenate([upright(raw[:, k : k + GROUP]) for k in range(0, raw.shape[1], GROUP)], axis=0)
+    v = raw + bias_ref[...]
     dt = jnp.maximum(v, 0.0) + jnp.log(1.0 + jnp.exp(-jnp.abs(v)))
     return dt, -dt * jnp.exp(dlog_ref[...])
 
@@ -223,8 +234,9 @@
 
 def fused_kernel(
     n,
-    x_ref,
-    gate_ref,
+    parts,
+    x_hbm,
+    gate_hbm,
     logit_ref,
     write_ref,
     read_ref,
@@ -235,84 +247,121 @@
     starts_ref,
     order_ref,
     out_ref,
-    fin,
-    fout,
+    x_ref,
+    gate_ref,
+    pair_out,
+    pair_in,
     total_s,
     decay_s,
+    e_in,
+    f_out,
+    back,
+    entry,
     made,
-    got,
     stage,
     final,
+    squares,
+    order_own,
+    order_all,
+    order_s,
+    load_sem,
+    pair_send,
+    pair_recv,
     chain_send,
     chain_recv,
+    back_send,
+    back_recv,
     send1,
     recv1,
     send2,
     recv2,
     send3,
     recv3,
-    order_all,
-    order_s,
     order_sem,
-    *scratch,
+    *rest,
 ):
+    got, scratch = rest[:parts], rest[parts:]
     cum_s, dt_s, write_t = scratch[:3]
-    groups = cum_s.shape[0]
+    groups, chunks = cum_s.shape[:2]
+    piece = stage.shape[-1]
+    per = WIDE // piece
+    steps = chunks // parts
+    state_size = write_t.shape[1]
     me = lax.axis_index("ctx")
-    offsets = range(1, n)
+    side = me % 2
+    level = me // 2
+    levels = n // 2
+    buddy = me + 1 - 2 * side
     half = n // 2
     mine = (me // half) * half
     other = half - mine
+    span = chunks // parts * WIDE
 
     def partner(k):
         far = 1 - k % 2
         return far * other + (1 - far) * mine + lax.rem(me + k // 2, half)
 
+    def send(source, target, sends, recvs, there):
+        return pltpu.make_async_remote_copy(
+            src_ref=source,
+            dst_ref=target,
+            send_sem=sends,
+            recv_sem=recvs,
+            device_id={"ctx": there},
+            device_id_type=pl.DeviceIdType.MESH,
+        )
+
+    def load(which, j):
+        cols = pl.ds(j * span, span)
+        source, target = ((x_hbm, x_ref), (gate_hbm, gate_ref))[which]
+        return pltpu.make_async_copy(source.at[:, cols], target.at[:, cols], load_sem.at[which, j])
+
+    def pair(c):
+        return send(pair_out.at[c], pair_in.at[c], pair_send.at[c], pair_recv.at[c], buddy)
+
+    def chain(c):
+        return send(f_out.at[c], e_in.at[c], chain_send.at[c], chain_recv.at[c], lax.rem(me + 2, n))
+
+    def give(c):
+        return send(back.at[c], entry.at[c], back_send.at[c], back_recv.at[c], buddy)
+
+    def order_to(there, slot):
+        return send(order_own, order_all.at[slot], send3.at[there], recv3.at[slot], there)
+
+    def first(there, slot, j):
+        return send(
+            made.at[there, j],
+            got[j].at[pl.ds(slot * groups, groups)],
+            send1.at[there, j],
+            recv1.at[slot, j],
+            there,
+        )
+
+    def second(there, slot, j):
+        return send(stage.at[there, j], final.at[slot, j], send2.at[there, j], recv2.at[slot, j], there)
+
+    for j in range(parts):
+        load(0, j).start()
+    for j in range(parts):
+        load(1, j).start()
     barrier = pltpu.get_barrier_semaphore()
     for off in range(1, n):
         pl.semaphore_signal(
             barrier, inc=1, device_id={"ctx": lax.rem(me + off, n)}, device_id_type=pl.DeviceIdType.MESH
         )
+    lane = lax.broadcasted_iota(jnp.int32, order_own.shape, 1)
+    held = jnp.zeros(order_own.shape, jnp.int32)
+    for g in range(groups):
+        held = jnp.where(lane == g, order_ref[g], held)
+    order_own[...] = held
+    order_all[me] = held
     gated_setup(logit_ref, bias_ref, dlog_ref, write_ref, read_ref, gain_ref, *scratch)
 
-    @pl.when(me == 0)
+    @pl.when(level == 0)
     def _():
-        fin[...] = jnp.zeros_like(fin)
-
-    def chain(c):
-        return pltpu.make_async_remote_copy(
-            src_ref=fout.at[c],
-            dst_ref=fin.at[c],
-            send_sem=chain_send.at[c],
-            recv_sem=chain_recv.at[c],
-            device_id={"ctx": lax.rem(me + 1, n)},
-            device_id_type=pl.DeviceIdType.MESH,
-        )
-
-    def spread_order(there, slot):
-        return pltpu.make_async_remote_copy(
-            src_ref=order_ref,
-            dst_ref=order_all.at[slot],
-            send_sem=send3.at[there],
-            recv_sem=recv3.at[slot],
-            device_id={"ctx": there},
-            device_id_type=pl.DeviceIdType.MESH,
-        )
-
-    def outward(source, target, sends, recvs, there, slot):
-        return pltpu.make_async_remote_copy(
-            src_ref=source.at[there],
-            dst_ref=target.at[pl.ds(slot * groups, groups)] if target is got else target.at[slot],
-            send_sem=sends.at[there],
-            recv_sem=recvs.at[slot],
-            device_id={"ctx": there},
-            device_id_type=pl.DeviceIdType.MESH,
-        )
+        e_in[...] = jnp.zeros_like(e_in)
 
     pl.semaphore_wait(barrier, n - 1)
-    order_all[me] = order_ref[...]
-    for off in offsets:
-        spread_order(lax.rem(me + off, n), me).start()
 
     def ends(c, carry):
         cols = pl.ds(pl.multiple_of(c * WIDE, WIDE), WIDE)
@@ -326,107 +375,180 @@
         total_s[c] = total
         decay_s[c] = jnp.broadcast_to(decay, (8, WIDE))
 
-        @pl.when(me == 0)
+        @pl.when(c % 2 != side)
         def _():
-            fout[c] = total.astype(jnp.bfloat16)
+            coarse = decay.astype(jnp.bfloat16).astype(jnp.float32)
+            row = lax.broadcasted_iota(jnp.int32, (EXTRA, WIDE), 0)
+            extra = jnp.where(row == 0, coarse, decay - coarse)
+            pair_out[c] = jnp.concatenate([total, extra], axis=0).astype(jnp.bfloat16)
+            pair(c).start()
+
+        return carry
+
+    for j in range(parts):
+        load(0, j).wait()
+        lax.fori_loop(j * steps, (j + 1) * steps, ends, 0)
+    for off in range(1, n):
+        order_to(lax.rem(me + off, n), me).start()
+
+    def relay(c):
+        pair(c).wait_recv()
+
+        @pl.when(level > 0)
+        def _():
+            chain(c).wait_recv()
+
+        state = e_in[c].astype(jnp.float32)
+        their = pair_in[c, :state_size].astype(jnp.float32)
+        tail = pair_in[c, state_size : state_size + EXTRA].astype(jnp.float32)
+        fade = tail[0:1] + tail[1:2]
+        total, decay = total_s[c], decay_s[c][0:1]
+        early = side == 0
+        middle = jnp.where(early, decay, fade) * state + jnp.where(early, total, their)
+
+        @pl.when(level < levels - 1)
+        def _():
+            end = jnp.where(early, fade, decay) * middle + jnp.where(early, their, total)
+            f_out[c] = end.astype(jnp.bfloat16)
             chain(c).start()
 
+        back[c] = jnp.where(early, middle, state).astype(jnp.bfloat16)
+        give(c).start()
+        entry[c] = jnp.where(early, state, middle).astype(jnp.bfloat16)
+
+    def part(j, carry):
+        def links(i, inner):
+            relay(j * steps + 2 * i + side)
+            return inner
+
+        lax.fori_loop(0, steps // 2, links, 0)
+        for s in range(parts):
+
+            @pl.when(j == s)
+            def _():
+                load(1, s).wait()
+
+        def one(t, inner):
+            i = lax.rem(t + me, steps)
+            c = j * steps + i
+
+            @pl.when(c % 2 != side)
+            def _():
+                give(c).wait_recv()
+
+            def put(g, value):
+                for p in range(per):
+                    made[p * steps + i, j, g] = value[:, p * piece : (p + 1) * piece]
+
+            gated_chunk(
+                c, entry[c].astype(jnp.float32), put, x_ref, gate_ref, read_ref, starts_ref, *scratch
+            )
+            for p in range(per):
+                there = p * steps + i
+                for s in range(parts):
+
+                    @pl.when(jnp.logical_and(j == s, there != me))
+                    def _():
+                        first(there, me, s).start()
+
+                    @pl.when(jnp.logical_and(j == s, there == me))
+                    def _():
+                        for g in range(groups):
+                            got[s][me * groups + g] = made[there, s, g]
+
+            return inner
+
+        lax.fori_loop(0, steps, one, 0)
         return carry
 
-    lax.fori_loop(0, n, ends, 0)
-
-    def relay(c, carry):
-        chain(c).wait_recv()
-
-        @pl.when(me < n - 1)
-        def _():
-            state = fin[c].astype(jnp.float32)
-            fout[c] = (decay_s[c][0:1] * state + total_s[c]).astype(jnp.bfloat16)
-            chain(c).start()
-
-        return carry
-
-    @pl.when(me > 0)
-    def _():
-        lax.fori_loop(0, n, relay, 0)
-
-    def one(k, carry):
-        c = partner(k)
-        state = fin[c].astype(jnp.float32)
-
-        def put(g, value):
-            made[c, g] = value
-
-        gated_chunk(c, state, put, x_ref, gate_ref, read_ref, starts_ref, *scratch)
-
-        @pl.when(c != me)
-        def _():
-            outward(made, got, send1, recv1, c, me).start()
-
-        @pl.when(c == me)
-        def _():
-            for g in range(groups):
-                got[me * groups + g] = made[c, g]
-
-        return carry
-
-    lax.fori_loop(0, n, one, 0)
-    for off in offsets:
+    lax.fori_loop(0, parts, part, 0)
+    for off in range(1, n):
         there = lax.rem(me + off, n)
-        spread_order(there, there).wait_recv()
+        order_to(there, there).wait_recv()
     fetch = pltpu.make_async_copy(order_all, order_s, order_sem)
     fetch.start()
     fetch.wait()
-    for off in offsets:
+    for j in range(parts):
+        for off in range(1, n):
+            there = lax.rem(me + off, n)
+            first(there, there, j).wait_recv()
+
+        def pick(k, carry, j=j):
+            there = partner(k)
+
+            @pl.when(there != me)
+            def _():
+                for g in range(groups):
+                    stage[there, j, g] = got[j][order_s[there, 0, g]]
+                second(there, me, j).start()
+
+            @pl.when(there == me)
+            def _():
+                for g in range(groups):
+                    final[me, j, g] = got[j][order_s[me, 0, g]]
+
+            return carry
+
+        lax.fori_loop(0, n, pick, 0)
+    squares[...] = jnp.zeros_like(squares)
+    tile = 32
+    for j in range(parts):
+        for off in range(1, n):
+            there = lax.rem(me + off, n)
+            second(there, there, j).wait_recv()
+        for g in range(groups):
+
+            def add(r, carry, j=j, g=g):
+                at = pl.ds(pl.multiple_of(r * tile, tile), tile)
+                total = squares[g, at, :]
+                for s in range(n):
+                    v = final[s, j, g, at, :].astype(jnp.float32)
+                    v = v * v
+                    for q in range(0, piece, 128):
+                        total = total + v[:, q : q + 128]
+                squares[g, at, :] = total
+                return carry
+
+            lax.fori_loop(0, GROUP // tile, add, 0)
+    for g in range(groups):
+
+        def norm(r, carry, g=g):
+            at = pl.ds(pl.multiple_of(r * tile, tile), tile)
+            into = pl.ds(pl.multiple_of(g * GROUP + r * tile, tile), tile)
+            total = jnp.sum(squares[g, at, :], axis=1, keepdims=True)
+            scale = lax.rsqrt(total * (1.0 / out_ref.shape[1]) + 1e-05)
+            for j in range(parts):
+                for s in range(n):
+                    v = final[s, j, g, at, :].astype(jnp.float32)
+                    low = (j * steps + s % steps) * WIDE + s // steps * piece
+                    w = weight_ref[:, low : low + piece]
+                    out_ref[into, low : low + piece] = (v * scale * w).astype(jnp.bfloat16)
+            return carry
+
+        lax.fori_loop(0, GROUP // tile, norm, 0)
+
+    def settle(c, carry):
+        @pl.when(c % 2 != side)
+        def _():
+            pair(c).wait_send()
+
+        @pl.when(c % 2 == side)
+        def _():
+            give(c).wait_send()
+
+            @pl.when(level < levels - 1)
+            def _():
+                chain(c).wait_send()
+
+        return carry
+
+    lax.fori_loop(0, chunks, settle, 0)
+    for off in range(1, n):
         there = lax.rem(me + off, n)
-        outward(made, got, send1, recv1, there, there).wait_recv()
-
-    def second(k, carry):
-        there = partner(k)
-        for g in range(groups):
-            stage[there, g] = got[order_s[there, 0, g]]
-
-        @pl.when(there != me)
-        def _():
-            outward(stage, final, send2, recv2, there, me).start()
-
-        return carry
-
-    lax.fori_loop(0, n, second, 0)
-    for g in range(groups):
-        final[me, g] = stage[me, g]
-
-    @pl.when(me < n - 1)
-    def _():
-        for c in range(n):
-            chain(c).wait_send()
-
-    for off in offsets:
-        there = lax.rem(me + off, n)
-        outward(made, got, send1, recv1, there, there).wait_send()
-        outward(stage, final, send2, recv2, there, there).wait_send()
-        spread_order(there, there).wait_send()
-    for off in offsets:
-        there = lax.rem(me + off, n)
-        outward(stage, final, send2, recv2, there, there).wait_recv()
-    tile = 32
-    for g in range(groups):
-
-        def norm(r, carry):
-            at = pl.ds(pl.multiple_of(r * tile, tile), tile)
-            total = jnp.zeros((tile, 1), jnp.float32)
-            for s in range(n):
-                v = final[s, g, at, :].astype(jnp.float32)
-                total = total + jnp.sum(v * v, axis=1, keepdims=True)
-            scale = lax.rsqrt(total * (1.0 / (n * WIDE)) + 1e-05)
-            for s in range(n):
-                v = final[s, g, at, :].astype(jnp.float32)
-                w = weight_ref[:, s * WIDE : (s + 1) * WIDE]
-                into = pl.ds(pl.multiple_of(g * GROUP + r * tile, tile), tile)
-                out_ref[into, s * WIDE : (s + 1) * WIDE] = (v * scale * w).astype(jnp.bfloat16)
-            return carry
-
-        lax.fori_loop(0, GROUP // tile, norm, 0)
+        order_to(there, there).wait_send()
+        for j in range(parts):
+            first(there, there, j).wait_send()
+            second(there, there, j).wait_send()
 
 
 def norm_kernel(in_ref, weight_ref, out_ref):
@@ -495,40 +617,52 @@
             v = v.transpose(1, 0, 2).reshape(1, v.shape[1], features)
         return v
 
-    if width == WIDE and devices % 2 == 0:
-        order = jnp.broadcast_to(jnp.pad(block_order, (0, 128 - groups))[None], (8, 128))
-        slab = (devices, groups, GROUP, WIDE)
+    piece = width // PARTS
+    per = max(WIDE // max(piece, 1), 1)
+    if width == 512 and devices % (2 * per) == 0:
+        slab = (devices, PARTS, groups, GROUP, piece)
+        state = (chunks, state_size, WIDE)
+        sems = pltpu.SemaphoreType.DMA
         return pl.pallas_call(
-            functools.partial(fused_kernel, devices),
+            functools.partial(fused_kernel, devices, PARTS),
             out_shape=jax.ShapeDtypeStruct((rows, features), jnp.bfloat16),
-            in_specs=[VM] * 9 + [SM, VM],
+            in_specs=[ANY] * 2 + [VM] * 7 + [SM] * 2,
             out_specs=VM,
             scratch_shapes=[
-                pltpu.VMEM((devices, state_size, WIDE), jnp.bfloat16),
-                pltpu.VMEM((devices, state_size, WIDE), jnp.bfloat16),
-                pltpu.VMEM((devices, state_size, WIDE), jnp.float32),
-                pltpu.VMEM((devices, 8, WIDE), jnp.float32),
-                pltpu.VMEM(slab, jnp.bfloat16),
-                pltpu.VMEM((devices * groups, GROUP, WIDE), jnp.bfloat16),
+                pltpu.VMEM((rows, features), jnp.bfloat16),
+                pltpu.VMEM((rows, features), jnp.bfloat16),
+                pltpu.VMEM((chunks, state_size + EXTRA, WIDE), jnp.bfloat16),
+                pltpu.VMEM((chunks, state_size + EXTRA, WIDE), jnp.bfloat16),
+                pltpu.VMEM(state, jnp.float32),
+                pltpu.VMEM((chunks, 8, WIDE), jnp.float32),
+                pltpu.VMEM(state, jnp.bfloat16),
+                pltpu.VMEM(state, jnp.bfloat16),
+                pltpu.VMEM(state, jnp.bfloat16),
+                pltpu.VMEM(state, jnp.bfloat16),
                 pltpu.VMEM(slab, jnp.bfloat16),
                 pltpu.VMEM(slab, jnp.bfloat16),
-            ]
-            + [pltpu.SemaphoreType.DMA((devices,))] * 8
-            + [
+                pltpu.VMEM(slab, jnp.bfloat16),
+                pltpu.VMEM((groups, GROUP, 128), jnp.float32),
+                pltpu.VMEM((8, 128), jnp.int32),
                 pltpu.VMEM((devices, 8, 128), jnp.int32),
                 pltpu.SMEM((devices, 8, 128), jnp.int32),
-                pltpu.SemaphoreType.DMA,
+                sems((2, PARTS)),
             ]
+            + [sems((chunks,))] * 6
+            + [sems((devices, PARTS))] * 4
+            + [sems((devices,))] * 2
+            + [sems]
+            + [pltpu.VMEM((devices * groups, GROUP, piece), jnp.bfloat16)] * PARTS
             + common
             + more,
             compiler_params=pltpu.CompilerParams(
-                collective_id=0, has_side_effects=True, vmem_limit_bytes=56 * 1024 * 1024
+                collective_id=0, has_side_effects=True, vmem_limit_bytes=60 * 1024 * 1024
             ),
             name="fused",
         )(
             head_input,
             gate_input,
-            increment_preactivation,
+            increment_preactivation.T,
             write_vector,
             read_vector,
             bias,
@@ -536,7 +670,7 @@
             gain,
             norm_weight.reshape(1, -1),
             doc_starts,
-            order,
+            block_order,
         )
 
     ends = pl.pallas_call(
@@ -547,7 +681,7 @@
         scratch_shapes=common,
         compiler_params=limit,
         name="end_states",
-    )(head_input, increment_preactivation, write_vector, bias, dlog, doc_starts, block_order)
+    )(head_input, increment_preactivation.T, write_vector, bias, dlog, doc_starts, block_order)
     ends = to_owners(ends)
     all_order = ends[:, state_size + 2, :groups].astype(jnp.int32).reshape(-1)
     entry = pl.pallas_call(
@@ -571,7 +705,7 @@
     )(
         head_input,
         gate_input,
-        increment_preactivation,
+        increment_preactivation.T,
         write_vector,
         read_vector,
         entry,

time: 173 us -> 147 us (0.85)
  Pallas kernels: 167 us -> 144 us
  local copies, waits for them, and re-layouts: 5.88 us -> 3.13 us
    pallas_call x1, Pallas kernels: 167 us -> 144 us  [local(): pl.pallas_call(functools.partial(fused_kernel, devices, PARTS), out_shape...]
    unnamed x2 -> x1, local copies, waits for them, and re-layouts: 4.62 us -> 3.13 us
where the time goes in v1:
time: 147 us
  Pallas kernels  144 us (98%)
  local copies, waits for them, and re-layouts  3.13 us (2%)
    pallas_call x1, Pallas kernels, local(): pl.pallas_call(functools.partial(fused_kernel, devices, PARTS), out_shape...  144 us
    unnamed x1, local copies, waits for them, and re-layouts  3.13 us

profile of v1, /device:TPU:0, one launch (start us, length us, event | category | flops | bytes accessed | tf_op | source)
XLA Modules:
  0.0 146.7 jit_solution(5506245289320803253)
XLA Ops:
  0.0 143.5 %fused.1 = bf16[256,4096]{1,0:T(8,128)(2,1)} custom-call(bf16[256,4096]{1,0:T(8,128)(2,1)} %x_hbm.1, bf16[256,4096]{1,0:T(8,128)(2,1)} %gate_hbm.1, bf16[64,256]{1,0:T(8,128)(2,1)} %bitcast.5, bf16[256,128]{1,0:T(8,128)(2,1)} %write_ref.1, bf16[256,128]{1,0:T(8,128)(2,1)} %read_ref.1, f32[1,64]{1,0:T(1,128)} %bitcast.7, f32[1,64]{1,0:T(1,128)} %bitcast.8, ...), custom_call_target="tpu_custom_call" | custom-call | tf_op jit(solution)/shard_map/fused/pallas_call | solution.py:626
  143.5 3.1 %copy.13 = bf16[256,4096]{1,0:T(8,128)(2,1)} copy(bf16[256,4096]{1,0:T(8,128)(2,1)} %fused.1) | data formatting | bytes 4194304

commit v2 on v1

--- a/solution.py
+++ b/solution.py
@@ -13,11 +13,13 @@
 WIDE = CHUNK * HEAD_DIM
 EXTRA = 16
 PARTS = 4
+LIMIT = 61 * 1024 * 1024
+UNIT = 256
 
 highest = lax.Precision.HIGHEST
 VM = pl.BlockSpec(memory_space=pltpu.VMEM)
 SM = pl.BlockSpec(memory_space=pltpu.SMEM)
-ANY = pl.BlockSpec(memory_space=pl.ANY)
+ANY = pl.BlockSpec(memory_space=pltpu.HBM)
 
 
 def transposed(v):
@@ -243,10 +245,10 @@
     bias_ref,
     dlog_ref,
     gain_ref,
-    weight_ref,
     starts_ref,
     order_ref,
     out_ref,
+    squares,
     x_ref,
     gate_ref,
     pair_out,
@@ -260,7 +262,6 @@
     made,
     stage,
     final,
-    squares,
     order_own,
     order_all,
     order_s,
@@ -278,6 +279,7 @@
     send3,
     recv3,
     order_sem,
+    gate_sem,
     *rest,
 ):
     got, scratch = rest[:parts], rest[parts:]
@@ -292,14 +294,8 @@
     level = me // 2
     levels = n // 2
     buddy = me + 1 - 2 * side
-    half = n // 2
-    mine = (me // half) * half
-    other = half - mine
     span = chunks // parts * WIDE
-
-    def partner(k):
-        far = 1 - k % 2
-        return far * other + (1 - far) * mine + lax.rem(me + k // 2, half)
+    units = WIDE // UNIT
 
     def send(source, target, sends, recvs, there):
         return pltpu.make_async_remote_copy(
@@ -355,13 +351,16 @@
         held = jnp.where(lane == g, order_ref[g], held)
     order_own[...] = held
     order_all[me] = held
-    gated_setup(logit_ref, bias_ref, dlog_ref, write_ref, read_ref, gain_ref, *scratch)
+    with jax.named_scope("setup"):
+        gated_setup(logit_ref, bias_ref, dlog_ref, write_ref, read_ref, gain_ref, *scratch)
 
     @pl.when(level == 0)
     def _():
         e_in[...] = jnp.zeros_like(e_in)
 
-    pl.semaphore_wait(barrier, n - 1)
+    @pl.when(me == 0)
+    def _():
+        entry[...] = jnp.zeros_like(entry)
 
     def ends(c, carry):
         cols = pl.ds(pl.multiple_of(c * WIDE, WIDE), WIDE)
@@ -372,109 +371,212 @@
             factor = (1.0 - starts_ref[g].astype(jnp.float32)) * last
             total = state if total is None else factor * total + state
             decay = factor if decay is None else factor * decay
-        total_s[c] = total
-        decay_s[c] = jnp.broadcast_to(decay, (8, WIDE))
+        for u in range(units):
+            cut = slice(u * UNIT, (u + 1) * UNIT)
+            total_s[c * units + u] = total[:, cut]
+            decay_s[c * units + u] = jnp.broadcast_to(decay[:, cut], (8, UNIT))
 
         @pl.when(c % 2 != side)
         def _():
             coarse = decay.astype(jnp.bfloat16).astype(jnp.float32)
             row = lax.broadcasted_iota(jnp.int32, (EXTRA, WIDE), 0)
             extra = jnp.where(row == 0, coarse, decay - coarse)
-            pair_out[c] = jnp.concatenate([total, extra], axis=0).astype(jnp.bfloat16)
-            pair(c).start()
-
+            full = jnp.concatenate([total, extra], axis=0).astype(jnp.bfloat16)
+            for u in range(units):
+                pair_out[c * units + u] = full[:, u * UNIT : (u + 1) * UNIT]
+
+        return carry
+
+    def offer(i, carry):
+        c = 2 * i + 1 - side
+        for u in range(units):
+            pair(c * units + u).start()
         return carry
 
     for j in range(parts):
-        load(0, j).wait()
-        lax.fori_loop(j * steps, (j + 1) * steps, ends, 0)
-    for off in range(1, n):
-        order_to(lax.rem(me + off, n), me).start()
-
-    def relay(c):
-        pair(c).wait_recv()
+        with jax.named_scope("loadx"):
+            load(0, j).wait()
+        with jax.named_scope("ends"):
+            lax.fori_loop(j * steps, (j + 1) * steps, ends, 0)
+        if j == 0:
+            with jax.named_scope("barrier"):
+                pl.semaphore_wait(barrier, n - 1)
+            for off in range(1, n):
+                order_to(lax.rem(me + off, n), me).start()
+        lax.fori_loop(j * steps // 2, (j + 1) * steps // 2, offer, 0)
+
+    def relay(q):
+        pair(q).wait_recv()
 
         @pl.when(level > 0)
         def _():
-            chain(c).wait_recv()
-
-        state = e_in[c].astype(jnp.float32)
-        their = pair_in[c, :state_size].astype(jnp.float32)
-        tail = pair_in[c, state_size : state_size + EXTRA].astype(jnp.float32)
+            chain(q).wait_recv()
+
+        state = e_in[q].astype(jnp.float32)
+        their = pair_in[q, :state_size].astype(jnp.float32)
+        tail = pair_in[q, state_size : state_size + EXTRA].astype(jnp.float32)
         fade = tail[0:1] + tail[1:2]
-        total, decay = total_s[c], decay_s[c][0:1]
+        total, decay = total_s[q], decay_s[q][0:1]
         early = side == 0
         middle = jnp.where(early, decay, fade) * state + jnp.where(early, total, their)
 
         @pl.when(level < levels - 1)
         def _():
             end = jnp.where(early, fade, decay) * middle + jnp.where(early, their, total)
-            f_out[c] = end.astype(jnp.bfloat16)
-            chain(c).start()
-
-        back[c] = jnp.where(early, middle, state).astype(jnp.bfloat16)
-        give(c).start()
-        entry[c] = jnp.where(early, state, middle).astype(jnp.bfloat16)
-
-    def part(j, carry):
-        def links(i, inner):
-            relay(j * steps + 2 * i + side)
-            return inner
-
-        lax.fori_loop(0, steps // 2, links, 0)
+            f_out[q] = end.astype(jnp.bfloat16)
+            chain(q).start()
+
+        @pl.when(me != 1)
+        def _():
+            back[q] = jnp.where(early, middle, state).astype(jnp.bfloat16)
+            give(q).start()
+
+        entry[q] = jnp.where(early, state, middle).astype(jnp.bfloat16)
+
+    def links(i, carry):
+        q = (2 * (i // units) + side) * units + i % units
+        relay(q)
+        return carry
+
+    inward = steps // 2 * units
+
+    low = level < levels // 2
+
+    def by_distance(k):
+        return jnp.where(low, levels - 1 - k, k)
+
+    def gate_ready(j):
         for s in range(parts):
 
             @pl.when(j == s)
             def _():
                 load(1, s).wait()
 
+    def compute(j, i):
+        c = j * steps + i
+
+        def put(g, value):
+            for p in range(per):
+                made[p * steps + i, j, g] = value[:, p * piece : (p + 1) * piece]
+
+        with jax.named_scope("gated"):
+            state = jnp.concatenate([entry[c * units + u].astype(jnp.float32) for u in range(units)], axis=1)
+            gated_chunk(c, state, put, x_ref, gate_ref, read_ref, starts_ref, *scratch)
+
+    def outward(j, there, wanted):
+        for s in range(parts):
+
+            @pl.when(jnp.logical_and(j == s, jnp.logical_and(there != me, wanted)))
+            def _():
+                first(there, me, s).start()
+
+    def keep(j, i):
+        for s in range(parts):
+
+            @pl.when(jnp.logical_and(j == s, lax.rem(me, steps) == i))
+            def _():
+                for g in range(groups):
+                    got[s][me * groups + g] = made[me, s, g]
+
+    def near_column(j, carry):
+        with jax.named_scope("links"):
+            lax.fori_loop(j * inward, (j + 1) * inward, links, 0)
+        gate_ready(j)
+
         def one(t, inner):
-            i = lax.rem(t + me, steps)
+            i = 2 * t + side
+            compute(j, i)
+            for k in range(per):
+                there = by_distance(k) * steps + i
+                outward(j, there, there // 2 < level)
+            keep(j, i)
+            return inner
+
+        lax.fori_loop(0, steps // 2, one, 0)
+        return carry
+
+    def postponed(far):
+        def some(j, carry):
+            def one(t, inner):
+                i = 2 * t + side
+                for k in range(per):
+                    there = by_distance(k) * steps + i
+                    high = there // 2
+                    outward(j, there, jnp.logical_and(high >= level, (high >= levels // 2) == far))
+                return inner
+
+            lax.fori_loop(0, steps // 2, one, 0)
+            return carry
+
+        lax.fori_loop(0, parts, some, 0)
+
+    def far_column(j, carry):
+        def one(t, inner):
+            i = 2 * t + 1 - side
             c = j * steps + i
 
-            @pl.when(c % 2 != side)
+            @pl.when(me > 0)
             def _():
-                give(c).wait_recv()
-
-            def put(g, value):
-                for p in range(per):
-                    made[p * steps + i, j, g] = value[:, p * piece : (p + 1) * piece]
-
-            gated_chunk(
-                c, entry[c].astype(jnp.float32), put, x_ref, gate_ref, read_ref, starts_ref, *scratch
-            )
-            for p in range(per):
-                there = p * steps + i
-                for s in range(parts):
-
-                    @pl.when(jnp.logical_and(j == s, there != me))
-                    def _():
-                        first(there, me, s).start()
-
-                    @pl.when(jnp.logical_and(j == s, there == me))
-                    def _():
-                        for g in range(groups):
-                            got[s][me * groups + g] = made[there, s, g]
-
+                with jax.named_scope("waitgive"):
+                    for u in range(units):
+                        give(c * units + u).wait_recv()
+
+            compute(j, i)
+            for k in range(per):
+                outward(j, by_distance(k) * steps + i, True)
+            keep(j, i)
             return inner
 
-        lax.fori_loop(0, steps, one, 0)
-        return carry
-
-    lax.fori_loop(0, parts, part, 0)
+        lax.fori_loop(0, steps // 2, one, 0)
+        return carry
+
+    lax.fori_loop(0, parts, near_column, 0)
+    for far in (False, True):
+        postponed(far)
+    lax.fori_loop(0, parts, far_column, 0)
+
+    def crossed(j, carry):
+        for k in range(n // 2):
+            there = jnp.where(low, n // 2, 0) + k
+            first(there, there, j).wait_send()
+        return carry
+
+    lower_inner = jnp.logical_and(level == levels // 2 - 1, level > 0)
+    upper_inner = jnp.logical_and(level == levels // 2, level < levels - 1)
+
+    @pl.when(jnp.logical_or(lower_inner, upper_inner))
+    def _():
+        with jax.named_scope("crossed"):
+            for j in range(parts):
+                crossed(j, 0)
+        pl.semaphore_signal(
+            gate_sem,
+            inc=1,
+            device_id={"ctx": jnp.where(low, me - 2, lax.rem(me + 2, n))},
+            device_id_type=pl.DeviceIdType.MESH,
+        )
+
     for off in range(1, n):
         there = lax.rem(me + off, n)
         order_to(there, there).wait_recv()
     fetch = pltpu.make_async_copy(order_all, order_s, order_sem)
     fetch.start()
     fetch.wait()
+    if levels > 2:
+
+        @pl.when(jnp.logical_or(level == levels // 2 - 2, level == levels // 2 + 1))
+        def _():
+            with jax.named_scope("gate"):
+                pl.semaphore_wait(gate_sem, 1)
+
     for j in range(parts):
-        for off in range(1, n):
-            there = lax.rem(me + off, n)
-            first(there, there, j).wait_recv()
+        with jax.named_scope("waitfirst"):
+            for off in range(1, n):
+                there = lax.rem(me + off, n)
+                first(there, there, j).wait_recv()
 
         def pick(k, carry, j=j):
-            there = partner(k)
+            there = 2 * by_distance(k // 2) + lax.rem(k + me, 2)
 
             @pl.when(there != me)
             def _():
@@ -489,66 +591,70 @@
 
             return carry
 
-        lax.fori_loop(0, n, pick, 0)
-    squares[...] = jnp.zeros_like(squares)
+        with jax.named_scope("pick"):
+            lax.fori_loop(0, n, pick, 0)
     tile = 32
     for j in range(parts):
-        for off in range(1, n):
-            there = lax.rem(me + off, n)
-            second(there, there, j).wait_recv()
-        for g in range(groups):
-
-            def add(r, carry, j=j, g=g):
+        with jax.named_scope("waitsecond"):
+            for off in range(1, n):
+                there = lax.rem(me + off, n)
+                second(there, there, j).wait_recv()
+
+        def add(r, carry, j=j):
+            for g in range(groups):
                 at = pl.ds(pl.multiple_of(r * tile, tile), tile)
-                total = squares[g, at, :]
+                into = pl.ds(pl.multiple_of(g * GROUP + r * tile, tile), tile)
+                total = jnp.zeros((tile, 128), jnp.float32) if j == 0 else squares[into, :]
                 for s in range(n):
-                    v = final[s, j, g, at, :].astype(jnp.float32)
+                    raw = final[s, j, g, at, :]
+                    left = (j * steps + s % steps) * WIDE + s // steps * piece
+                    out_ref[into, left : left + piece] = raw
+                    v = raw.astype(jnp.float32)
                     v = v * v
                     for q in range(0, piece, 128):
                         total = total + v[:, q : q + 128]
-                squares[g, at, :] = total
-                return carry
-
+                squares[into, :] = total
+            return carry
+
+        with jax.named_scope("add"):
             lax.fori_loop(0, GROUP // tile, add, 0)
-    for g in range(groups):
-
-        def norm(r, carry, g=g):
-            at = pl.ds(pl.multiple_of(r * tile, tile), tile)
-            into = pl.ds(pl.multiple_of(g * GROUP + r * tile, tile), tile)
-            total = jnp.sum(squares[g, at, :], axis=1, keepdims=True)
-            scale = lax.rsqrt(total * (1.0 / out_ref.shape[1]) + 1e-05)
+
+    def settle(i, carry):
+        pair((2 * (i // units) + 1 - side) * units + i % units).wait_send()
+        q = (2 * (i // units) + side) * units + i % units
+
+        @pl.when(me != 1)
+        def _():
+            give(q).wait_send()
+
+        @pl.when(level < levels - 1)
+        def _():
+            chain(q).wait_send()
+
+        return carry
+
+    with jax.named_scope("settle"):
+        lax.fori_loop(0, parts * inward, settle, 0)
+    with jax.named_scope("sent"):
+        for off in range(1, n):
+            there = lax.rem(me + off, n)
+            order_to(there, there).wait_send()
+            waited = jnp.logical_and(jnp.logical_or(lower_inner, upper_inner), (there < n // 2) != low)
             for j in range(parts):
-                for s in range(n):
-                    v = final[s, j, g, at, :].astype(jnp.float32)
-                    low = (j * steps + s % steps) * WIDE + s // steps * piece
-                    w = weight_ref[:, low : low + piece]
-                    out_ref[into, low : low + piece] = (v * scale * w).astype(jnp.bfloat16)
-            return carry
-
-        lax.fori_loop(0, GROUP // tile, norm, 0)
-
-    def settle(c, carry):
-        @pl.when(c % 2 != side)
-        def _():
-            pair(c).wait_send()
-
-        @pl.when(c % 2 == side)
-        def _():
-            give(c).wait_send()
-
-            @pl.when(level < levels - 1)
-            def _():
-                chain(c).wait_send()
-
-        return carry
-
-    lax.fori_loop(0, chunks, settle, 0)
-    for off in range(1, n):
-        there = lax.rem(me + off, n)
-        order_to(there, there).wait_send()
-        for j in range(parts):
-            first(there, there, j).wait_send()
-            second(there, there, j).wait_send()
+                second(there, there, j).wait_send()
+
+                @pl.when(jnp.logical_not(waited))
+                def _():
+                    first(there, there, j).wait_send()
+
+
+def scale_kernel(in_ref, squares_ref, weight_ref, out_ref):
+    total = jnp.sum(squares_ref[...], axis=1, keepdims=True)
+    scale = lax.rsqrt(total * (1.0 / in_ref.shape[1]) + 1e-05)
+    for q in range(0, in_ref.shape[1], WIDE):
+        cols = slice(q, q + WIDE)
+        v = in_ref[:, cols].astype(jnp.float32)
+        out_ref[:, cols] = (v * scale * weight_ref[:, cols]).astype(jnp.bfloat16)
 
 
 def norm_kernel(in_ref, weight_ref, out_ref):
@@ -619,22 +725,26 @@
 
     piece = width // PARTS
     per = max(WIDE // max(piece, 1), 1)
-    if width == 512 and devices % (2 * per) == 0:
+    if width == 512 and devices == 2 * per:
         slab = (devices, PARTS, groups, GROUP, piece)
-        state = (chunks, state_size, WIDE)
+        links = features // UNIT
+        state = (links, state_size, UNIT)
         sems = pltpu.SemaphoreType.DMA
-        return pl.pallas_call(
+        packed, squares = pl.pallas_call(
             functools.partial(fused_kernel, devices, PARTS),
-            out_shape=jax.ShapeDtypeStruct((rows, features), jnp.bfloat16),
-            in_specs=[ANY] * 2 + [VM] * 7 + [SM] * 2,
-            out_specs=VM,
+            out_shape=[
+                pltpu.VMEM((rows, features), jnp.bfloat16),
+                pltpu.VMEM((rows, 128), jnp.float32),
+            ],
+            in_specs=[ANY] * 2 + [VM] * 6 + [SM] * 2,
+            out_specs=[VM] * 2,
             scratch_shapes=[
                 pltpu.VMEM((rows, features), jnp.bfloat16),
                 pltpu.VMEM((rows, features), jnp.bfloat16),
-                pltpu.VMEM((chunks, state_size + EXTRA, WIDE), jnp.bfloat16),
-                pltpu.VMEM((chunks, state_size + EXTRA, WIDE), jnp.bfloat16),
+                pltpu.VMEM((links, state_size + EXTRA, UNIT), jnp.bfloat16),
+                pltpu.VMEM((links, state_size + EXTRA, UNIT), jnp.bfloat16),
                 pltpu.VMEM(state, jnp.float32),
-                pltpu.VMEM((chunks, 8, WIDE), jnp.float32),
+                pltpu.VMEM((links, 8, UNIT), jnp.float32),
                 pltpu.VMEM(state, jnp.bfloat16),
                 pltpu.VMEM(state, jnp.bfloat16),
                 pltpu.VMEM(state, jnp.bfloat16),
@@ -642,21 +752,20 @@
                 pltpu.VMEM(slab, jnp.bfloat16),
                 pltpu.VMEM(slab, jnp.bfloat16),
                 pltpu.VMEM(slab, jnp.bfloat16),
-                pltpu.VMEM((groups, GROUP, 128), jnp.float32),
                 pltpu.VMEM((8, 128), jnp.int32),
                 pltpu.VMEM((devices, 8, 128), jnp.int32),
                 pltpu.SMEM((devices, 8, 128), jnp.int32),
                 sems((2, PARTS)),
             ]
-            + [sems((chunks,))] * 6
+            + [sems((links,))] * 6
             + [sems((devices, PARTS))] * 4
             + [sems((devices,))] * 2
-            + [sems]
+            + [sems, pltpu.SemaphoreType.REGULAR]
             + [pltpu.VMEM((devices * groups, GROUP, piece), jnp.bfloat16)] * PARTS
             + common
             + more,
             compiler_params=pltpu.CompilerParams(
-                collective_id=0, has_side_effects=True, vmem_limit_bytes=60 * 1024 * 1024
+                collective_id=0, has_side_effects=True, vmem_limit_bytes=LIMIT
             ),
             name="fused",
         )(
@@ -668,10 +777,23 @@
             bias,
             dlog,
             gain,
-            norm_weight.reshape(1, -1),
             doc_starts,
             block_order,
         )
+        tile = 64
+        return pl.pallas_call(
+            scale_kernel,
+            grid=(rows // tile,),
+            out_shape=jax.ShapeDtypeStruct((rows, features), jnp.bfloat16),
+            in_specs=[
+                pl.BlockSpec((tile, features), lambda r: (r, 0)),
+                pl.BlockSpec((tile, 128), lambda r: (r, 0)),
+                pl.BlockSpec((1, features), lambda r: (0, 0)),
+            ],
+            out_specs=pl.BlockSpec((tile, features), lambda r: (r, 0)),
+            compiler_params=pltpu.CompilerParams(vmem_limit_bytes=8 * 1024 * 1024),
+            name="scale",
+        )(packed, squares, norm_weight.reshape(1, -1))
 
     ends = pl.pallas_call(
         state_kernel,

time: 147 us -> 121 us (0.82)
  the two profiles are of different devices: /device:TPU:0 before, /device:TPU:16 now
where the time goes in v2:
time: 121 us
  Pallas kernels  121 us (100%)
    pallas_call x1, Pallas kernels, local(): pl.pallas_call(functools.partial(fused_kernel, devices, PARTS), out_shape...  119 us

profile of v2, /device:TPU:16, one launch (start us, length us, event | category | flops | bytes accessed | tf_op | source)
XLA Modules:
  0.0 121.3 jit_solution(14968248464003347541)
XLA Ops:
  0.0 0.0 copy-start
  0.0 119.1 %fused.1 = (bf16[256,4096]{1,0:T(8,128)(2,1)S(1)}, f32[256,128]{1,0:T(8,128)S(1)}) custom-call(bf16[256,4096]{1,0:T(8,128)(2,1)} %x_hbm.1, bf16[256,4096]{1,0:T(8,128)(2,1)} %gate_hbm.1, bf16[64,256]{1,0:T(8,128)(2,1)} %bitcast.6, bf16[256,128]{1,0:T(8,128)(2,1)} %write_ref.1, bf16[256,128]{1,0:T(8,128)(2,1)} %read_ref.1, f32[1,64]{1,0:T(1,128)} %bitcast.7, ...), custom_call_target="tpu_custom_call" | custom-call | tf_op jit(solution)/shard_map/fused/pallas_call | solution.py:733
  119.1 0.0 copy-done
  119.1 2.2 %scale.1 = bf16[256,4096]{1,0:T(8,128)(2,1)} custom-call(bf16[256,4096]{1,0:T(8,128)(2,1)S(1)} %get-tuple-element.7.in_ref, f32[256,128]{1,0:T(8,128)S(1)} %get-tuple-element.8.squares_ref, f32[1,4096]{1,0:T(1,128)S(1)} %bitcast.5), custom_call_target="tpu_custom_call" | custom-call | tf_op jit(solution)/shard_map/scale/pallas_call | solution.py:784
Async XLA Ops:
  0.0 119.1 %copy-start = (f32[4096]{0:T(1024)S(1)}, f32[4096]{0:T(1024)}, u32[]{:S(2)}) copy-start(f32[4096]{0:T(1024)} %param.19) | copy-start | bytes 49156

commit v3 on v2

--- a/solution.py
+++ b/solution.py
@@ -14,7 +14,7 @@
 EXTRA = 16
 PARTS = 4
 LIMIT = 61 * 1024 * 1024
-UNIT = 256
+UNIT = 128
 
 highest = lax.Precision.HIGHEST
 VM = pl.BlockSpec(memory_space=pltpu.VMEM)
@@ -156,6 +156,7 @@
         score_s[g] = jnp.where(mask, score, 0.0)
     for c in range(chunks):
         gain_s[c] = jnp.broadcast_to(gain_ref[:, c * CHUNK : (c + 1) * CHUNK], (8, CHUNK))
+    return cums
 
 
 def gated_chunk(
@@ -253,12 +254,16 @@
     gate_ref,
     pair_out,
     pair_in,
+    fade_out,
+    fade_in,
+    fade_s,
     total_s,
     decay_s,
     e_in,
     f_out,
     back,
-    entry,
+    near_entry,
+    far_entry,
     made,
     stage,
     final,
@@ -266,12 +271,10 @@
     order_all,
     order_s,
     load_sem,
-    pair_send,
-    pair_recv,
-    chain_send,
-    chain_recv,
-    back_send,
-    back_recv,
+    link_recv,
+    link_send,
+    fade_send,
+    fade_recv,
     send1,
     recv1,
     send2,
@@ -287,15 +290,15 @@
     groups, chunks = cum_s.shape[:2]
     piece = stage.shape[-1]
     per = WIDE // piece
-    steps = chunks // parts
-    state_size = write_t.shape[1]
+    units = WIDE // UNIT
+    span = 2 * WIDE
     me = lax.axis_index("ctx")
     side = me % 2
     level = me // 2
     levels = n // 2
+    half = n // 2
     buddy = me + 1 - 2 * side
-    span = chunks // parts * WIDE
-    units = WIDE // UNIT
+    low = level < levels // 2
 
     def send(source, target, sends, recvs, there):
         return pltpu.make_async_remote_copy(
@@ -307,34 +310,37 @@
             device_id_type=pl.DeviceIdType.MESH,
         )
 
+    def landed(ref, sem):
+        send(ref, ref, sem, sem, buddy).wait_recv()
+
+    def left(ref, sem):
+        send(ref, ref, sem, sem, buddy).wait_send()
+
     def load(which, j):
         cols = pl.ds(j * span, span)
         source, target = ((x_hbm, x_ref), (gate_hbm, gate_ref))[which]
         return pltpu.make_async_copy(source.at[:, cols], target.at[:, cols], load_sem.at[which, j])
 
-    def pair(c):
-        return send(pair_out.at[c], pair_in.at[c], pair_send.at[c], pair_recv.at[c], buddy)
-
-    def chain(c):
-        return send(f_out.at[c], e_in.at[c], chain_send.at[c], chain_recv.at[c], lax.rem(me + 2, n))
-
-    def give(c):
-        return send(back.at[c], entry.at[c], back_send.at[c], back_recv.at[c], buddy)
-
-    def order_to(there, slot):
-        return send(order_own, order_all.at[slot], send3.at[there], recv3.at[slot], there)
-
-    def first(there, slot, j):
+    def pair(r):
+        return send(pair_out.at[r], pair_in.at[r], link_send.at[0], link_recv.at[0, r], buddy)
+
+    def chain(r):
+        return send(f_out.at[r], e_in.at[r], link_send.at[1], link_recv.at[1, r], lax.rem(me + 2, n))
+
+    def give(r):
+        return send(back.at[r], far_entry.at[r], link_send.at[2], link_recv.at[2, r], buddy)
+
+    def fade():
+        return send(fade_out, fade_in, fade_send, fade_recv, buddy)
+
+    def first(there, j):
+        far = ((there < half) != low).astype(jnp.int32)
         return send(
-            made.at[there, j],
-            got[j].at[pl.ds(slot * groups, groups)],
-            send1.at[there, j],
-            recv1.at[slot, j],
-            there,
+            made.at[there, j], got[j].at[pl.ds(me * groups, groups)], send1.at[far], recv1.at[j], there
         )
 
-    def second(there, slot, j):
-        return send(stage.at[there, j], final.at[slot, j], send2.at[there, j], recv2.at[slot, j], there)
+    def second(there, j):
+        return send(stage.at[there, j], final.at[me, j], send2, recv2.at[j], there)
 
     for j in range(parts):
         load(0, j).start()
@@ -345,14 +351,21 @@
         pl.semaphore_signal(
             barrier, inc=1, device_id={"ctx": lax.rem(me + off, n)}, device_id_type=pl.DeviceIdType.MESH
         )
-    lane = lax.broadcasted_iota(jnp.int32, order_own.shape, 1)
-    held = jnp.zeros(order_own.shape, jnp.int32)
-    for g in range(groups):
-        held = jnp.where(lane == g, order_ref[g], held)
-    order_own[...] = held
-    order_all[me] = held
     with jax.named_scope("setup"):
-        gated_setup(logit_ref, bias_ref, dlog_ref, write_ref, read_ref, gain_ref, *scratch)
+        lane = lax.broadcasted_iota(jnp.int32, order_own.shape, 1)
+        held = jnp.zeros(order_own.shape, jnp.int32)
+        for g in range(groups):
+            held = jnp.where(lane == g, order_ref[g], held)
+        order_own[...] = held
+        order_all[me] = held
+        cums = gated_setup(logit_ref, bias_ref, dlog_ref, write_ref, read_ref, gain_ref, *scratch)
+        heads = bias_ref.shape[1]
+        whole = None
+        for g in range(groups):
+            factor = (1.0 - starts_ref[g].astype(jnp.float32)) * jnp.exp(cums[g][GROUP - 1 : GROUP])
+            whole = factor if whole is None else whole * factor
+        whole = jnp.concatenate([whole, jnp.zeros((1, 128 - heads), jnp.float32)], axis=1)
+        fade_out[...] = jnp.broadcast_to(whole, (8, 128))
 
     @pl.when(level == 0)
     def _():
@@ -360,7 +373,7 @@
 
     @pl.when(me == 0)
     def _():
-        entry[...] = jnp.zeros_like(entry)
+        far_entry[...] = jnp.zeros_like(far_entry)
 
     def ends(c, carry):
         cols = pl.ds(pl.multiple_of(c * WIDE, WIDE), WIDE)
@@ -371,76 +384,90 @@
             factor = (1.0 - starts_ref[g].astype(jnp.float32)) * last
             total = state if total is None else factor * total + state
             decay = factor if decay is None else factor * decay
+        base = c // 2 * units
+
+        @pl.when(c % 2 == side)
+        def _():
+            for u in range(units):
+                cut = slice(u * UNIT, (u + 1) * UNIT)
+                total_s[base + u] = total[:, cut]
+                decay_s[base + u] = jnp.broadcast_to(decay[:, cut], (8, UNIT))
+
+        @pl.when(c % 2 != side)
+        def _():
+            for u in range(units):
+                pair_out[base + u] = total[:, u * UNIT : (u + 1) * UNIT].astype(jnp.bfloat16)
+
+        return carry
+
+    def relay(r, carry):
+        pair(r).wait_recv()
+
+        @pl.when(level > 0)
+        def _():
+            chain(r).wait_recv()
+
+        state = e_in[r].astype(jnp.float32)
+        their = pair_in[r].astype(jnp.float32)
+        theirs = fade_s[r][0:1]
+        total, decay = total_s[r], decay_s[r][0:1]
+        early = side == 0
+        middle = jnp.where(early, decay, theirs) * state + jnp.where(early, total, their)
+
+        @pl.when(level < levels - 1)
+        def _():
+            end = jnp.where(early, theirs, decay) * middle + jnp.where(early, their, total)
+            f_out[r] = end.astype(jnp.bfloat16)
+            chain(r).start()
+
+        @pl.when(me != 1)
+        def _():
+            back[r] = jnp.where(early, middle, state).astype(jnp.bfloat16)
+            give(r).start()
+
+        near_entry[r] = jnp.where(early, state, middle).astype(jnp.bfloat16)
+        return carry
+
+    def links(j):
+        with jax.named_scope("links"):
+            lax.fori_loop(j * units, (j + 1) * units, relay, 0)
+
+    def offer(j):
         for u in range(units):
-            cut = slice(u * UNIT, (u + 1) * UNIT)
-            total_s[c * units + u] = total[:, cut]
-            decay_s[c * units + u] = jnp.broadcast_to(decay[:, cut], (8, UNIT))
-
-        @pl.when(c % 2 != side)
-        def _():
-            coarse = decay.astype(jnp.bfloat16).astype(jnp.float32)
-            row = lax.broadcasted_iota(jnp.int32, (EXTRA, WIDE), 0)
-            extra = jnp.where(row == 0, coarse, decay - coarse)
-            full = jnp.concatenate([total, extra], axis=0).astype(jnp.bfloat16)
-            for u in range(units):
-                pair_out[c * units + u] = full[:, u * UNIT : (u + 1) * UNIT]
-
-        return carry
-
-    def offer(i, carry):
-        c = 2 * i + 1 - side
-        for u in range(units):
-            pair(c * units + u).start()
-        return carry
-
+            pair(j * units + u).start()
+
+    ahead = parts // 2
     for j in range(parts):
-        with jax.named_scope("loadx"):
-            load(0, j).wait()
-        with jax.named_scope("ends"):
-            lax.fori_loop(j * steps, (j + 1) * steps, ends, 0)
-        if j == 0:
+        load(0, j).wait()
+        if j == ahead:
             with jax.named_scope("barrier"):
                 pl.semaphore_wait(barrier, n - 1)
+            fade().start()
+            for k in range(ahead):
+                offer(k)
             for off in range(1, n):
-                order_to(lax.rem(me + off, n), me).start()
-        lax.fori_loop(j * steps // 2, (j + 1) * steps // 2, offer, 0)
-
-    def relay(q):
-        pair(q).wait_recv()
-
-        @pl.when(level > 0)
-        def _():
-            chain(q).wait_recv()
-
-        state = e_in[q].astype(jnp.float32)
-        their = pair_in[q, :state_size].astype(jnp.float32)
-        tail = pair_in[q, state_size : state_size + EXTRA].astype(jnp.float32)
-        fade = tail[0:1] + tail[1:2]
-        total, decay = total_s[q], decay_s[q][0:1]
-        early = side == 0
-        middle = jnp.where(early, decay, fade) * state + jnp.where(early, total, their)
-
-        @pl.when(level < levels - 1)
-        def _():
-            end = jnp.where(early, fade, decay) * middle + jnp.where(early, their, total)
-            f_out[q] = end.astype(jnp.bfloat16)
-            chain(q).start()
-
-        @pl.when(me != 1)
-        def _():
-            back[q] = jnp.where(early, middle, state).astype(jnp.bfloat16)
-            give(q).start()
-
-        entry[q] = jnp.where(early, state, middle).astype(jnp.bfloat16)
-
-    def links(i, carry):
-        q = (2 * (i // units) + side) * units + i % units
-        relay(q)
-        return carry
-
-    inward = steps // 2 * units
-
-    low = level < levels // 2
+                there = lax.rem(me + off, n)
+                send(order_own, order_all.at[me], send3, recv3, there).start()
+        with jax.named_scope("ends"):
+            ends(2 * j + 1 - side, 0)
+        if j >= ahead:
+            offer(j)
+        with jax.named_scope("ends"):
+            ends(2 * j + side, 0)
+    fade().wait_recv()
+    tile = fade_in[0:1, :]
+    for c in range(chunks):
+
+        @pl.when(c % 2 == side)
+        def _(c=c):
+            lanes = spread(tile[:, c * CHUNK : (c + 1) * CHUNK])
+            for u in range(units):
+                fade_s[c // 2 * units + u] = jnp.broadcast_to(lanes[:, u * UNIT : (u + 1) * UNIT], (8, UNIT))
+
+    @pl.when(low)
+    def _():
+        with jax.named_scope("linksall"):
+            lax.fori_loop(0, parts * units, relay, 0)
 
     def by_distance(k):
         return jnp.where(low, levels - 1 - k, k)
@@ -452,103 +479,70 @@
             def _():
                 load(1, s).wait()
 
-    def compute(j, i):
-        c = j * steps + i
-
+    def compute(j, i, entry):
         def put(g, value):
             for p in range(per):
-                made[p * steps + i, j, g] = value[:, p * piece : (p + 1) * piece]
+                made[2 * p + i, j, g] = value[:, p * piece : (p + 1) * piece]
 
         with jax.named_scope("gated"):
-            state = jnp.concatenate([entry[c * units + u].astype(jnp.float32) for u in range(units)], axis=1)
-            gated_chunk(c, state, put, x_ref, gate_ref, read_ref, starts_ref, *scratch)
+            state = jnp.concatenate([entry[j * units + u].astype(jnp.float32) for u in range(units)], axis=1)
+            gated_chunk(2 * j + i, state, put, x_ref, gate_ref, read_ref, starts_ref, *scratch)
 
     def outward(j, there, wanted):
         for s in range(parts):
 
             @pl.when(jnp.logical_and(j == s, jnp.logical_and(there != me, wanted)))
             def _():
-                first(there, me, s).start()
-
-    def keep(j, i):
+                first(there, s).start()
+
+    def near_column(j, carry):
+        @pl.when(jnp.logical_not(low))
+        def _():
+            links(j)
+
+        gate_ready(j)
+        compute(j, side, near_entry)
+        for k in range(per):
+            there = 2 * k + side
+            outward(j, there, jnp.logical_or(low, k < level))
         for s in range(parts):
 
-            @pl.when(jnp.logical_and(j == s, lax.rem(me, steps) == i))
+            @pl.when(j == s)
             def _():
                 for g in range(groups):
                     got[s][me * groups + g] = made[me, s, g]
 
-    def near_column(j, carry):
-        with jax.named_scope("links"):
-            lax.fori_loop(j * inward, (j + 1) * inward, links, 0)
-        gate_ready(j)
-
-        def one(t, inner):
-            i = 2 * t + side
-            compute(j, i)
-            for k in range(per):
-                there = by_distance(k) * steps + i
-                outward(j, there, there // 2 < level)
-            keep(j, i)
-            return inner
-
-        lax.fori_loop(0, steps // 2, one, 0)
         return carry
 
-    def postponed(far):
-        def some(j, carry):
-            def one(t, inner):
-                i = 2 * t + side
-                for k in range(per):
-                    there = by_distance(k) * steps + i
-                    high = there // 2
-                    outward(j, there, jnp.logical_and(high >= level, (high >= levels // 2) == far))
-                return inner
-
-            lax.fori_loop(0, steps // 2, one, 0)
-            return carry
-
-        lax.fori_loop(0, parts, some, 0)
+    def postponed(j, carry):
+        for k in range(per):
+            outward(j, 2 * k + side, jnp.logical_not(jnp.logical_or(low, k < level)))
+        return carry
 
     def far_column(j, carry):
-        def one(t, inner):
-            i = 2 * t + 1 - side
-            c = j * steps + i
-
-            @pl.when(me > 0)
-            def _():
-                with jax.named_scope("waitgive"):
-                    for u in range(units):
-                        give(c * units + u).wait_recv()
-
-            compute(j, i)
-            for k in range(per):
-                outward(j, by_distance(k) * steps + i, True)
-            keep(j, i)
-            return inner
-
-        lax.fori_loop(0, steps // 2, one, 0)
+        @pl.when(me > 0)
+        def _():
+            with jax.named_scope("waitgive"):
+                for u in range(units):
+                    give(j * units + u).wait_recv()
+
+        compute(j, 1 - side, far_entry)
+        for k in range(per):
+            outward(j, 2 * by_distance(k) + 1 - side, True)
         return carry
 
     lax.fori_loop(0, parts, near_column, 0)
-    for far in (False, True):
-        postponed(far)
+    lax.fori_loop(0, parts, postponed, 0)
     lax.fori_loop(0, parts, far_column, 0)
-
-    def crossed(j, carry):
-        for k in range(n // 2):
-            there = jnp.where(low, n // 2, 0) + k
-            first(there, there, j).wait_send()
-        return carry
 
     lower_inner = jnp.logical_and(level == levels // 2 - 1, level > 0)
     upper_inner = jnp.logical_and(level == levels // 2, level < levels - 1)
-
-    @pl.when(jnp.logical_or(lower_inner, upper_inner))
+    inner = jnp.logical_or(lower_inner, upper_inner)
+
+    @pl.when(inner)
     def _():
         with jax.named_scope("crossed"):
-            for j in range(parts):
-                crossed(j, 0)
+            left(made.at[pl.ds(0, half)], send1.at[1])
         pl.semaphore_signal(
             gate_sem,
             inc=1,
@@ -556,9 +550,7 @@
             device_id_type=pl.DeviceIdType.MESH,
         )
 
-    for off in range(1, n):
-        there = lax.rem(me + off, n)
-        order_to(there, there).wait_recv()
+    landed(order_all.at[pl.ds(0, n - 1)], recv3)
     fetch = pltpu.make_async_copy(order_all, order_s, order_sem)
     fetch.start()
     fetch.wait()
@@ -571,18 +563,16 @@
 
     for j in range(parts):
         with jax.named_scope("waitfirst"):
-            for off in range(1, n):
-                there = lax.rem(me + off, n)
-                first(there, there, j).wait_recv()
+            landed(got[j].at[pl.ds(0, (n - 1) * groups)], recv1.at[j])
 
         def pick(k, carry, j=j):
-            there = 2 * by_distance(k // 2) + lax.rem(k + me, 2)
+            there = 2 * lax.rem(k // 2 + jnp.where(low, levels // 2, 0), levels) + lax.rem(k + me, 2)
 
             @pl.when(there != me)
             def _():
                 for g in range(groups):
                     stage[there, j, g] = got[j][order_s[there, 0, g]]
-                second(there, me, j).start()
+                second(there, j).start()
 
             @pl.when(there == me)
             def _():
@@ -596,9 +586,7 @@
     tile = 32
     for j in range(parts):
         with jax.named_scope("waitsecond"):
-            for off in range(1, n):
-                there = lax.rem(me + off, n)
-                second(there, there, j).wait_recv()
+            landed(final.at[pl.ds(0, n - 1), j], recv2.at[j])
 
         def add(r, carry, j=j):
             for g in range(groups):
@@ -607,8 +595,8 @@
                 total = jnp.zeros((tile, 128), jnp.float32) if j == 0 else squares[into, :]
                 for s in range(n):
                     raw = final[s, j, g, at, :]
-                    left = (j * steps + s % steps) * WIDE + s // steps * piece
-                    out_ref[into, left : left + piece] = raw
+                    start = (2 * j + s % 2) * WIDE + s // 2 * piece
+                    out_ref[into, start : start + piece] = raw
                     v = raw.astype(jnp.float32)
                     v = v * v
                     for q in range(0, piece, 128):
@@ -619,42 +607,47 @@
         with jax.named_scope("add"):
             lax.fori_loop(0, GROUP // tile, add, 0)
 
-    def settle(i, carry):
-        pair((2 * (i // units) + 1 - side) * units + i % units).wait_send()
-        q = (2 * (i // units) + side) * units + i % units
+    with jax.named_scope("sent"):
+        left(pair_out, link_send.at[0])
+        left(fade_out, fade_send)
+
+        @pl.when(level < levels - 1)
+        def _():
+            left(f_out, link_send.at[1])
 
         @pl.when(me != 1)
         def _():
-            give(q).wait_send()
-
-        @pl.when(level < levels - 1)
-        def _():
-            chain(q).wait_send()
-
-        return carry
-
-    with jax.named_scope("settle"):
-        lax.fori_loop(0, parts * inward, settle, 0)
-    with jax.named_scope("sent"):
-        for off in range(1, n):
-            there = lax.rem(me + off, n)
-            order_to(there, there).wait_send()
-            waited = jnp.logical_and(jnp.logical_or(lower_inner, upper_inner), (there < n // 2) != low)
-            for j in range(parts):
-                second(there, there, j).wait_send()
-
-                @pl.when(jnp.logical_not(waited))
-                def _():
-                    first(there, there, j).wait_send()
-
-
-def scale_kernel(in_ref, squares_ref, weight_ref, out_ref):
-    total = jnp.sum(squares_ref[...], axis=1, keepdims=True)
-    scale = lax.rsqrt(total * (1.0 / in_ref.shape[1]) + 1e-05)
-    for q in range(0, in_ref.shape[1], WIDE):
-        cols = slice(q, q + WIDE)
-        v = in_ref[:, cols].astype(jnp.float32)
-        out_ref[:, cols] = (v * scale * weight_ref[:, cols]).astype(jnp.bfloat16)
+            left(back, link_send.at[2])
+
+        left(order_all.at[pl.ds(0, n - 1)], send3)
+        left(made.at[pl.ds(0, half - 1)], send1.at[0])
+
+        @pl.when(jnp.logical_not(inner))
+        def _():
+            left(made.at[pl.ds(0, half)], send1.at[1])
+
+        left(stage.at[pl.ds(0, n - 1)], send2)
+
+
+def scale_kernel(in_ref, squares_ref, weight_ref, out_hbm, ready, sem):
+    rows, width = in_ref.shape
+    tile = rows // sem.shape[0]
+
+    def push(r):
+        at = pl.ds(r * tile, tile)
+        return pltpu.make_async_copy(ready.at[at, :], out_hbm.at[at, :], sem.at[r])
+
+    for r in range(sem.shape[0]):
+        at = slice(r * tile, (r + 1) * tile)
+        total = jnp.sum(squares_ref[at, :], axis=1, keepdims=True)
+        scale = lax.rsqrt(total * (1.0 / width) + 1e-05)
+        for q in range(0, width, WIDE):
+            cols = slice(q, q + WIDE)
+            v = in_ref[at, cols].astype(jnp.float32)
+            ready[at, cols] = (v * scale * weight_ref[:, cols]).astype(jnp.bfloat16)
+        push(r).start()
+    for r in range(sem.shape[0]):
+        push(r).wait()
 
 
 def norm_kernel(in_ref, weight_ref, out_ref):
@@ -725,9 +718,9 @@
 
     piece = width // PARTS
     per = max(WIDE // max(piece, 1), 1)
-    if width == 512 and devices == 2 * per:
+    if width == 512 and devices == 2 * per and chunks == 2 * PARTS:
         slab = (devices, PARTS, groups, GROUP, piece)
-        links = features // UNIT
+        links = features // UNIT // 2
         state = (links, state_size, UNIT)
         sems = pltpu.SemaphoreType.DMA
         packed, squares = pl.pallas_call(
@@ -741,26 +734,34 @@
             scratch_shapes=[
                 pltpu.VMEM((rows, features), jnp.bfloat16),
                 pltpu.VMEM((rows, features), jnp.bfloat16),
-                pltpu.VMEM((links, state_size + EXTRA, UNIT), jnp.bfloat16),
-                pltpu.VMEM((links, state_size + EXTRA, UNIT), jnp.bfloat16),
+                pltpu.VMEM(state, jnp.bfloat16),
+                pltpu.VMEM(state, jnp.bfloat16),
+                pltpu.VMEM((8, 128), jnp.float32),
+                pltpu.VMEM((8, 128), jnp.float32),
+                pltpu.VMEM((links, 8, UNIT), jnp.float32),
                 pltpu.VMEM(state, jnp.float32),
                 pltpu.VMEM((links, 8, UNIT), jnp.float32),
-                pltpu.VMEM(state, jnp.bfloat16),
-                pltpu.VMEM(state, jnp.bfloat16),
-                pltpu.VMEM(state, jnp.bfloat16),
-                pltpu.VMEM(state, jnp.bfloat16),
-                pltpu.VMEM(slab, jnp.bfloat16),
-                pltpu.VMEM(slab, jnp.bfloat16),
-                pltpu.VMEM(slab, jnp.bfloat16),
+            ]
+            + [pltpu.VMEM(state, jnp.bfloat16)] * 5
+            + [pltpu.VMEM(slab, jnp.bfloat16)] * 3
+            + [
                 pltpu.VMEM((8, 128), jnp.int32),
                 pltpu.VMEM((devices, 8, 128), jnp.int32),
                 pltpu.SMEM((devices, 8, 128), jnp.int32),
                 sems((2, PARTS)),
+                sems((3, links)),
+                sems((3,)),
+                sems,
+                sems,
+                sems((2,)),
+                sems((PARTS,)),
+                sems,
+                sems((PARTS,)),
+                sems,
+                sems,
+                sems,
+                pltpu.SemaphoreType.REGULAR,
             ]
-            + [sems((links,))] * 6
-            + [sems((devices, PARTS))] * 4
-            + [sems((devices,))] * 2
-            + [sems, pltpu.SemaphoreType.REGULAR]
             + [pltpu.VMEM((devices * groups, GROUP, piece), jnp.bfloat16)] * PARTS
             + common
             + more,
@@ -780,17 +781,12 @@
             doc_starts,
             block_order,
         )
-        tile = 64
         return pl.pallas_call(
             scale_kernel,
-            grid=(rows // tile,),
             out_shape=jax.ShapeDtypeStruct((rows, features), jnp.bfloat16),
-            in_specs=[
-                pl.BlockSpec((tile, features), lambda r: (r, 0)),
-                pl.BlockSpec((tile, 128), lambda r: (r, 0)),
-                pl.BlockSpec((1, features), lambda r: (0, 0)),
-            ],
-            out_specs=pl.BlockSpec((tile, features), lambda r: (r, 0)),
+            in_specs=[VM] * 3,
+            out_specs=ANY,
+            scratch_shapes=[pltpu.VMEM((rows, features), jnp.bfloat16), sems((4,))],
             compiler_params=pltpu.CompilerParams(vmem_limit_bytes=8 * 1024 * 1024),
             name="scale",
         )(packed, squares, norm_weight.reshape(1, -1))

time: 121 us -> 116 us (0.959)
  the two profiles are of different devices: /device:TPU:16 before, /device:TPU:25 now
where the time goes in v3:
time: 116 us
  Pallas kernels  116 us (100%)
    pallas_call x1, Pallas kernels, local(): pl.pallas_call(functools.partial(fused_kernel, devices, PARTS), out_shape...  115 us

profile of v3, /device:TPU:25, one launch (start us, length us, event | category | flops | bytes accessed | tf_op | source)
XLA Modules:
  0.0 116.3 jit_solution(7067821896604095228)
XLA Ops:
  0.0 0.0 copy-start
  0.0 114.7 %fused.1 = (bf16[256,4096]{1,0:T(8,128)(2,1)S(1)}, f32[256,128]{1,0:T(8,128)S(1)}) custom-call(bf16[256,4096]{1,0:T(8,128)(2,1)} %x_hbm.1, bf16[256,4096]{1,0:T(8,128)(2,1)} %gate_hbm.1, bf16[64,256]{1,0:T(8,128)(2,1)} %bitcast.6, bf16[256,128]{1,0:T(8,128)(2,1)} %write_ref.1, bf16[256,128]{1,0:T(8,128)(2,1)} %read_ref.1, f32[1,64]{1,0:T(1,128)} %bitcast.7, ...), custom_call_target="tpu_custom_call" | custom-call | tf_op jit(solution)/shard_map/fused/pallas_call | solution.py:726
  114.7 0.0 copy-done
  114.7 1.6 %scale.1 = bf16[256,4096]{1,0:T(8,128)(2,1)} custom-call(bf16[256,4096]{1,0:T(8,128)(2,1)S(1)} %get-tuple-element.7.in_ref, f32[256,128]{1,0:T(8,128)S(1)} %get-tuple-element.8.squares_ref, f32[1,4096]{1,0:T(1,128)S(1)} %bitcast.5), custom_call_target="tpu_custom_call" | custom-call | tf_op jit(solution)/shard_map/scale/pallas_call | solution.py:784
Async XLA Ops:
  0.0 114.7 %copy-start = (f32[4096]{0:T(1024)S(1)}, f32[4096]{0:T(1024)}, u32[]{:S(2)}) copy-start(f32[4096]{0:T(1024)} %param.19) | copy-start | bytes 49156

commit v4 on v3

--- a/solution.py
+++ b/solution.py
@@ -142,8 +142,12 @@
 def gated_setup(
     logit_ref, bias_ref, dlog_ref, write_ref, read_ref, gain_ref, cum_s, dt_s, write_t, cum_t, dt_t, gain_s, score_s
 ):
+    dt, cums = prepare(logit_ref, bias_ref, dlog_ref, write_ref, cum_s, dt_s, write_t)
+    score_setup(dt, cums, read_ref, gain_ref, cum_s, write_t, cum_t, dt_t, gain_s, score_s)
+
+
+def score_setup(dt, cums, read_ref, gain_ref, cum_s, write_t, cum_t, dt_t, gain_s, score_s):
     groups, chunks = cum_s.shape[:2]
-    dt, cums = prepare(logit_ref, bias_ref, dlog_ref, write_ref, cum_s, dt_s, write_t)
     mask = lower_mask()
     for g in range(groups):
         rows = slice(g * GROUP, (g + 1) * GROUP)
@@ -156,7 +160,6 @@
         score_s[g] = jnp.where(mask, score, 0.0)
     for c in range(chunks):
         gain_s[c] = jnp.broadcast_to(gain_ref[:, c * CHUNK : (c + 1) * CHUNK], (8, CHUNK))
-    return cums
 
 
 def gated_chunk(
@@ -272,6 +275,7 @@
     order_s,
     load_sem,
     link_recv,
+    give_recv,
     link_send,
     fade_send,
     fade_recv,
@@ -283,6 +287,8 @@
     recv3,
     order_sem,
     gate_sem,
+    ready_sem,
+    side_sem,
     *rest,
 ):
     got, scratch = rest[:parts], rest[parts:]
@@ -328,7 +334,7 @@
         return send(f_out.at[r], e_in.at[r], link_send.at[1], link_recv.at[1, r], lax.rem(me + 2, n))
 
     def give(r):
-        return send(back.at[r], far_entry.at[r], link_send.at[2], link_recv.at[2, r], buddy)
+        return send(back.at[r], far_entry.at[r], link_send.at[2], give_recv.at[r // units], buddy)
 
     def fade():
         return send(fade_out, fade_in, fade_send, fade_recv, buddy)
@@ -347,10 +353,27 @@
     for j in range(parts):
         load(1, j).start()
     barrier = pltpu.get_barrier_semaphore()
-    for off in range(1, n):
-        pl.semaphore_signal(
-            barrier, inc=1, device_id={"ctx": lax.rem(me + off, n)}, device_id_type=pl.DeviceIdType.MESH
-        )
+
+    def tell(sem, there):
+        pl.semaphore_signal(sem, inc=1, device_id={"ctx": there}, device_id_type=pl.DeviceIdType.MESH)
+
+    above = level < levels - 1
+    below = level > 0
+    tell(barrier, buddy)
+
+    @pl.when(above)
+    def _():
+        tell(barrier, lax.rem(me + 2, n))
+
+    @pl.when(below)
+    def _():
+        tell(barrier, lax.rem(me + n - 2, n))
+
+    def send_orders():
+        for off in range(1, n):
+            there = lax.rem(me + off, n)
+            send(order_own, order_all.at[me], send3, recv3, there).start()
+
     with jax.named_scope("setup"):
         lane = lax.broadcasted_iota(jnp.int32, order_own.shape, 1)
         held = jnp.zeros(order_own.shape, jnp.int32)
@@ -358,7 +381,7 @@
             held = jnp.where(lane == g, order_ref[g], held)
         order_own[...] = held
         order_all[me] = held
-        cums = gated_setup(logit_ref, bias_ref, dlog_ref, write_ref, read_ref, gain_ref, *scratch)
+        dt, cums = prepare(logit_ref, bias_ref, dlog_ref, write_ref, cum_s, dt_s, write_t)
         heads = bias_ref.shape[1]
         whole = None
         for g in range(groups):
@@ -436,24 +459,64 @@
         for u in range(units):
             pair(j * units + u).start()
 
-    ahead = parts // 2
-    for j in range(parts):
-        load(0, j).wait()
-        if j == ahead:
-            with jax.named_scope("barrier"):
-                pl.semaphore_wait(barrier, n - 1)
-            fade().start()
-            for k in range(ahead):
-                offer(k)
-            for off in range(1, n):
-                there = lax.rem(me + off, n)
-                send(order_own, order_all.at[me], send3, recv3, there).start()
+    def hear_above():
+        with jax.named_scope("ready"):
+            pl.semaphore_wait(ready_sem, 1)
+
+    def swap_half(j):
         with jax.named_scope("ends"):
             ends(2 * j + 1 - side, 0)
-        if j >= ahead:
-            offer(j)
+        if j == 0:
+            with jax.named_scope("barrier"):
+                pl.semaphore_wait(barrier, 1 + above.astype(jnp.int32) + below.astype(jnp.int32))
+            fade().start()
+        offer(j)
+
+    def keep_half(j):
         with jax.named_scope("ends"):
             ends(2 * j + side, 0)
+
+    def by_distance(k):
+        return jnp.where(low, levels - 1 - k, k)
+
+    def gate_ready(j):
+        for s in range(parts):
+
+            @pl.when(j == s)
+            def _():
+                load(1, s).wait()
+
+    def compute(j, i, entry):
+        def put(g, value):
+            for p in range(per):
+                made[2 * p + i, j, g] = value[:, p * piece : (p + 1) * piece]
+
+        with jax.named_scope("gated"):
+            state = jnp.concatenate([entry[j * units + u].astype(jnp.float32) for u in range(units)], axis=1)
+            gated_chunk(2 * j + i, state, put, x_ref, gate_ref, read_ref, starts_ref, *scratch)
+
+    def outward(j, there, wanted):
+        for s in range(parts):
+
+            @pl.when(jnp.logical_and(j == s, jnp.logical_and(there != me, wanted)))
+            def _():
+                first(there, s).start()
+
+    late = parts - 1
+    for j in range(late):
+        load(0, j).wait()
+        swap_half(j)
+        if j == 0:
+
+            @pl.when(jnp.logical_and(below, level == levels - 2))
+            def _():
+                tell(ready_sem, me - 2)
+
+            with jax.named_scope("scores"):
+                score_setup(dt, cums, read_ref, gain_ref, cum_s, write_t, *scratch[3:])
+        if j == 1:
+            keep_half(0)
+            keep_half(1)
     fade().wait_recv()
     tile = fade_in[0:1, :]
     for c in range(chunks):
@@ -464,47 +527,55 @@
             for u in range(units):
                 fade_s[c // 2 * units + u] = jnp.broadcast_to(lanes[:, u * UNIT : (u + 1) * UNIT], (8, UNIT))
 
+    @pl.when(jnp.logical_and(below, level < levels - 2))
+    def _():
+        hear_above()
+        tell(ready_sem, me - 2)
+
+    @pl.when(low)
+    def _():
+        links(0)
+
+    bottom = jnp.logical_and(level == 0, levels > 2)
+
+    @pl.when(bottom)
+    def _():
+        hear_above()
+        load(1, 0).wait()
+        compute(0, side, near_entry)
+        for k in range(per):
+            outward(0, 2 * k + side, k >= levels // 2)
+
+    load(0, late).wait()
+    swap_half(late)
+    for j in range(2, parts):
+        keep_half(j)
+
     @pl.when(low)
     def _():
         with jax.named_scope("linksall"):
-            lax.fori_loop(0, parts * units, relay, 0)
-
-    def by_distance(k):
-        return jnp.where(low, levels - 1 - k, k)
-
-    def gate_ready(j):
-        for s in range(parts):
-
-            @pl.when(j == s)
-            def _():
-                load(1, s).wait()
-
-    def compute(j, i, entry):
-        def put(g, value):
-            for p in range(per):
-                made[2 * p + i, j, g] = value[:, p * piece : (p + 1) * piece]
-
-        with jax.named_scope("gated"):
-            state = jnp.concatenate([entry[j * units + u].astype(jnp.float32) for u in range(units)], axis=1)
-            gated_chunk(2 * j + i, state, put, x_ref, gate_ref, read_ref, starts_ref, *scratch)
-
-    def outward(j, there, wanted):
-        for s in range(parts):
-
-            @pl.when(jnp.logical_and(j == s, jnp.logical_and(there != me, wanted)))
-            def _():
-                first(there, s).start()
+            lax.fori_loop(units, parts * units, relay, 0)
+
+        tell(side_sem, buddy)
+
 
     def near_column(j, carry):
         @pl.when(jnp.logical_not(low))
         def _():
             links(j)
 
-        gate_ready(j)
-        compute(j, side, near_entry)
+        begun = jnp.logical_and(bottom, j == 0)
+
+        @pl.when(jnp.logical_not(begun))
+        def _():
+            gate_ready(j)
+            compute(j, side, near_entry)
+
         for k in range(per):
-            there = 2 * k + side
-            outward(j, there, jnp.logical_or(low, k < level))
+            there = 2 * by_distance(k) + side
+            high = there // 2
+            fresh = jnp.logical_not(jnp.logical_and(begun, high >= levels // 2))
+            outward(j, there, jnp.logical_and(fresh, jnp.logical_or(low, high < level)))
         for s in range(parts):
 
             @pl.when(j == s)
@@ -523,8 +594,11 @@
         @pl.when(me > 0)
         def _():
             with jax.named_scope("waitgive"):
-                for u in range(units):
-                    give(j * units + u).wait_recv()
+                landed(far_entry.at[pl.ds(j * units, units)], give_recv.at[j])
+
+        @pl.when(jnp.logical_and(j == 0, jnp.logical_not(low)))
+        def _():
+            send_orders()
 
         compute(j, 1 - side, far_entry)
         for k in range(per):
@@ -533,6 +607,12 @@
 
     lax.fori_loop(0, parts, near_column, 0)
     lax.fori_loop(0, parts, postponed, 0)
+
+    @pl.when(low)
+    def _():
+        pl.semaphore_wait(side_sem, 1)
+        send_orders()
+
     lax.fori_loop(0, parts, far_column, 0)
 
     lower_inner = jnp.logical_and(level == levels // 2 - 1, level > 0)
@@ -566,7 +646,7 @@
             landed(got[j].at[pl.ds(0, (n - 1) * groups)], recv1.at[j])
 
         def pick(k, carry, j=j):
-            there = 2 * lax.rem(k // 2 + jnp.where(low, levels // 2, 0), levels) + lax.rem(k + me, 2)
+            there = 2 * by_distance(k // 2) + lax.rem(k + 1 + me, 2)
 
             @pl.when(there != me)
             def _():
@@ -749,7 +829,8 @@
                 pltpu.VMEM((devices, 8, 128), jnp.int32),
                 pltpu.SMEM((devices, 8, 128), jnp.int32),
                 sems((2, PARTS)),
-                sems((3, links)),
+                sems((2, links)),
+                sems((PARTS,)),
                 sems((3,)),
                 sems,
                 sems,
@@ -760,8 +841,8 @@
                 sems,
                 sems,
                 sems,
-                pltpu.SemaphoreType.REGULAR,
             ]
+            + [pltpu.SemaphoreType.REGULAR] * 3
             + [pltpu.VMEM((devices * groups, GROUP, piece), jnp.bfloat16)] * PARTS
             + common
             + more,

time: 116 us -> 114 us (0.983)
  the two profiles are of different devices: /device:TPU:25 before, /device:TPU:16 now
where the time goes in v4:
time: 114 us
  Pallas kernels  114 us (100%)
    pallas_call x1, Pallas kernels, local(): pl.pallas_call(functools.partial(fused_kernel, devices, PARTS), out_shape...  112 us

profile of v4, /device:TPU:16, one launch (start us, length us, event | category | flops | bytes accessed | tf_op | source)
XLA Modules:
  0.0 114.0 jit_solution(6951329893402333041)
XLA Ops:
  0.0 0.0 copy-start
  0.0 112.4 %fused.1 = (bf16[256,4096]{1,0:T(8,128)(2,1)S(1)}, f32[256,128]{1,0:T(8,128)S(1)}) custom-call(bf16[256,4096]{1,0:T(8,128)(2,1)} %x_hbm.1, bf16[256,4096]{1,0:T(8,128)(2,1)} %gate_hbm.1, bf16[64,256]{1,0:T(8,128)(2,1)} %bitcast.6, bf16[256,128]{1,0:T(8,128)(2,1)} %write_ref.1, bf16[256,128]{1,0:T(8,128)(2,1)} %read_ref.1, f32[1,64]{1,0:T(1,128)} %bitcast.7, ...), custom_call_target="tpu_custom_call" | custom-call | tf_op jit(solution)/shard_map/fused/pallas_call | solution.py:806
  112.4 0.0 copy-done
  112.4 1.6 %scale.1 = bf16[256,4096]{1,0:T(8,128)(2,1)} custom-call(bf16[256,4096]{1,0:T(8,128)(2,1)S(1)} %get-tuple-element.7.in_ref, f32[256,128]{1,0:T(8,128)S(1)} %get-tuple-element.8.squares_ref, f32[1,4096]{1,0:T(1,128)S(1)} %bitcast.5), custom_call_target="tpu_custom_call" | custom-call | tf_op jit(solution)/shard_map/scale/pallas_call | solution.py:865
Async XLA Ops:
  0.0 112.4 %copy-start = (f32[4096]{0:T(1024)S(1)}, f32[4096]{0:T(1024)}, u32[]{:S(2)}) copy-start(f32[4096]{0:T(1024)} %param.19) | copy-start | bytes 49156

commit v5 on v4

--- a/solution.py
+++ b/solution.py
@@ -62,7 +62,15 @@
     )
 
 
-def prepare(logit_ref, bias_ref, dlog_ref, write_ref, cum_s, dt_s, write_t):
+def scatter(dt, cums, cum_s, dt_s, some):
+    for g in range(len(cums)):
+        rows = slice(g * GROUP, (g + 1) * GROUP)
+        for c in some:
+            cum_s[g, c] = cums[g][:, c * CHUNK : (c + 1) * CHUNK]
+            dt_s[g, c] = dt[rows, c * CHUNK : (c + 1) * CHUNK]
+
+
+def prepare(logit_ref, bias_ref, dlog_ref, write_ref, cum_s, dt_s, write_t, some=None):
     heads = bias_ref.shape[1]
     dt, fall = step_terms(logit_ref, bias_ref, dlog_ref)
     tri = lower_mask().astype(jnp.float32)
@@ -71,10 +79,8 @@
         rows = slice(g * GROUP, (g + 1) * GROUP)
         cum = jnp.dot(tri, fall[rows], precision=highest, preferred_element_type=jnp.float32)
         cums.append(cum)
-        for c in range(heads // CHUNK):
-            cum_s[g, c] = cum[:, c * CHUNK : (c + 1) * CHUNK]
-            dt_s[g, c] = dt[rows, c * CHUNK : (c + 1) * CHUNK]
         write_t[g] = write_ref[rows, :].astype(jnp.float32).T.astype(jnp.bfloat16)
+    scatter(dt, cums, cum_s, dt_s, range(heads // CHUNK) if some is None else some)
     return dt, cums
 
 
@@ -243,6 +249,16 @@
     parts,
     x_hbm,
     gate_hbm,
+    logit_hbm,
+    write_hbm,
+    read_hbm,
+    bias_hbm,
+    dlog_hbm,
+    gain_hbm,
+    starts_hbm,
+    order_hbm,
+    out_ref,
+    squares,
     logit_ref,
     write_ref,
     read_ref,
@@ -251,8 +267,7 @@
     gain_ref,
     starts_ref,
     order_ref,
-    out_ref,
-    squares,
+    small_sem,
     x_ref,
     gate_ref,
     pair_out,
@@ -348,26 +363,49 @@
     def second(there, j):
         return send(stage.at[there, j], final.at[me, j], send2, recv2.at[j], there)
 
-    for j in range(parts):
+    barrier = pltpu.get_barrier_semaphore()
+
+    def tell(sem, there):
+        pl.semaphore_signal(sem, inc=1, device_id={"ctx": there}, device_id_type=pl.DeviceIdType.MESH)
+
+    above = level < levels - 1
+    below = level > 0
+    tell(barrier, buddy)
+
+    @pl.when(above)
+    def _():
+        tell(barrier, lax.rem(me + 2, n))
+
+    @pl.when(below)
+    def _():
+        tell(barrier, lax.rem(me + n - 2, n))
+
+    small = [
+        pltpu.make_async_copy(source, target, small_sem.at[k])
+        for k, (source, target) in enumerate(
+            (
+                (logit_hbm, logit_ref),
+                (bias_hbm, bias_ref),
+                (dlog_hbm, dlog_ref),
+                (write_hbm, write_ref),
+                (starts_hbm, starts_ref),
+                (read_hbm, read_ref),
+                (gain_hbm, gain_ref),
+                (order_hbm, order_ref),
+            )
+        )
+    ]
+    for copy in small[:5]:
+        copy.start()
+    load(0, 0).start()
+    for copy in small[5:]:
+        copy.start()
+    for copy in small[:4]:
+        copy.wait()
+    for j in range(1, parts):
         load(0, j).start()
     for j in range(parts):
         load(1, j).start()
-    barrier = pltpu.get_barrier_semaphore()
-
-    def tell(sem, there):
-        pl.semaphore_signal(sem, inc=1, device_id={"ctx": there}, device_id_type=pl.DeviceIdType.MESH)
-
-    above = level < levels - 1
-    below = level > 0
-    tell(barrier, buddy)
-
-    @pl.when(above)
-    def _():
-        tell(barrier, lax.rem(me + 2, n))
-
-    @pl.when(below)
-    def _():
-        tell(barrier, lax.rem(me + n - 2, n))
 
     def send_orders():
         for off in range(1, n):
@@ -375,14 +413,9 @@
             send(order_own, order_all.at[me], send3, recv3, there).start()
 
     with jax.named_scope("setup"):
-        lane = lax.broadcasted_iota(jnp.int32, order_own.shape, 1)
-        held = jnp.zeros(order_own.shape, jnp.int32)
-        for g in range(groups):
-            held = jnp.where(lane == g, order_ref[g], held)
-        order_own[...] = held
-        order_all[me] = held
-        dt, cums = prepare(logit_ref, bias_ref, dlog_ref, write_ref, cum_s, dt_s, write_t)
+        dt, cums = prepare(logit_ref, bias_ref, dlog_ref, write_ref, cum_s, dt_s, write_t, range(2))
         heads = bias_ref.shape[1]
+        small[4].wait()
         whole = None
         for g in range(groups):
             factor = (1.0 - starts_ref[g].astype(jnp.float32)) * jnp.exp(cums[g][GROUP - 1 : GROUP])
@@ -513,6 +546,15 @@
                 tell(ready_sem, me - 2)
 
             with jax.named_scope("scores"):
+                for copy in small[5:]:
+                    copy.wait()
+                lane = lax.broadcasted_iota(jnp.int32, order_own.shape, 1)
+                held = jnp.zeros(order_own.shape, jnp.int32)
+                for g in range(groups):
+                    held = jnp.where(lane == g, order_ref[g], held)
+                order_own[...] = held
+                order_all[me] = held
+                scatter(dt, cums, cum_s, dt_s, range(2, chunks))
                 score_setup(dt, cums, read_ref, gain_ref, cum_s, write_t, *scratch[3:])
         if j == 1:
             keep_half(0)
@@ -619,21 +661,20 @@
     upper_inner = jnp.logical_and(level == levels // 2, level < levels - 1)
     inner = jnp.logical_or(lower_inner, upper_inner)
 
-    @pl.when(inner)
-    def _():
+    def crossed():
         with jax.named_scope("crossed"):
             left(made.at[pl.ds(0, half)], send1.at[1])
-        pl.semaphore_signal(
-            gate_sem,
-            inc=1,
-            device_id={"ctx": jnp.where(low, me - 2, lax.rem(me + 2, n))},
-            device_id_type=pl.DeviceIdType.MESH,
-        )
+        tell(gate_sem, jnp.where(low, me - 2, lax.rem(me + 2, n)))
 
     landed(order_all.at[pl.ds(0, n - 1)], recv3)
     fetch = pltpu.make_async_copy(order_all, order_s, order_sem)
     fetch.start()
     fetch.wait()
+
+    @pl.when(upper_inner)
+    def _():
+        crossed()
+
     if levels > 2:
 
         @pl.when(jnp.logical_or(level == levels // 2 - 2, level == levels // 2 + 1))
@@ -663,6 +704,12 @@
 
         with jax.named_scope("pick"):
             lax.fori_loop(0, n, pick, 0)
+        if j == parts - 2:
+
+            @pl.when(lower_inner)
+            def _():
+                crossed()
+
     tile = 32
     for j in range(parts):
         with jax.named_scope("waitsecond"):
@@ -809,9 +856,18 @@
                 pltpu.VMEM((rows, features), jnp.bfloat16),
                 pltpu.VMEM((rows, 128), jnp.float32),
             ],
-            in_specs=[ANY] * 2 + [VM] * 6 + [SM] * 2,
+            in_specs=[ANY] * 10,
             out_specs=[VM] * 2,
             scratch_shapes=[
+                pltpu.VMEM((heads, rows), jnp.bfloat16),
+                pltpu.VMEM((rows, state_size), jnp.bfloat16),
+                pltpu.VMEM((rows, state_size), jnp.bfloat16),
+                pltpu.VMEM((1, heads), jnp.float32),
+                pltpu.VMEM((1, heads), jnp.float32),
+                pltpu.VMEM((1, heads), jnp.float32),
+                pltpu.SMEM((groups,), jnp.int32),
+                pltpu.SMEM((groups,), jnp.int32),
+                sems((8,)),
                 pltpu.VMEM((rows, features), jnp.bfloat16),
                 pltpu.VMEM((rows, features), jnp.bfloat16),
                 pltpu.VMEM(state, jnp.bfloat16),

time: 114 us -> 114 us (level)
  no operation moved by 1% of the time
where the time goes in v5:
time: 114 us
  Pallas kernels  114 us (100%)
    pallas_call x1, Pallas kernels, local(): pl.pallas_call(functools.partial(fused_kernel, devices, PARTS), out_shape...  112 us

profile of v5, /device:TPU:16, one launch (start us, length us, event | category | flops | bytes accessed | tf_op | source)
XLA Modules:
  0.0 113.5 jit_solution(5594883333105431428)
XLA Ops:
  0.0 0.0 copy-start
  0.0 112.0 %fused.1 = (bf16[256,4096]{1,0:T(8,128)(2,1)S(1)}, f32[256,128]{1,0:T(8,128)S(1)}) custom-call(bf16[256,4096]{1,0:T(8,128)(2,1)} %x_hbm.1, bf16[256,4096]{1,0:T(8,128)(2,1)} %gate_hbm.1, bf16[64,256]{1,0:T(8,128)(2,1)} %bitcast.6, bf16[256,128]{1,0:T(8,128)(2,1)} %write_hbm.1, bf16[256,128]{1,0:T(8,128)(2,1)} %read_hbm.1, f32[1,64]{1,0:T(1,128)} %bitcast.7, ...), custom_call_target="tpu_custom_call" | custom-call | tf_op jit(solution)/shard_map/fused/pallas_call | solution.py:853
  112.0 0.0 copy-done
  112.0 1.6 %scale.1 = bf16[256,4096]{1,0:T(8,128)(2,1)} custom-call(bf16[256,4096]{1,0:T(8,128)(2,1)S(1)} %get-tuple-element.7.in_ref, f32[256,128]{1,0:T(8,128)S(1)} %get-tuple-element.8.squares_ref, f32[1,4096]{1,0:T(1,128)S(1)} %bitcast.5), custom_call_target="tpu_custom_call" | custom-call | tf_op jit(solution)/shard_map/scale/pallas_call | solution.py:921
Async XLA Ops:
  0.0 112.0 %copy-start = (f32[4096]{0:T(1024)S(1)}, f32[4096]{0:T(1024)}, u32[]{:S(2)}) copy-start(f32[4096]{0:T(1024)} %param.19) | copy-start | bytes 49156

commit v6 on v5

--- a/solution.py
+++ b/solution.py
@@ -421,7 +421,7 @@
             factor = (1.0 - starts_ref[g].astype(jnp.float32)) * jnp.exp(cums[g][GROUP - 1 : GROUP])
             whole = factor if whole is None else whole * factor
         whole = jnp.concatenate([whole, jnp.zeros((1, 128 - heads), jnp.float32)], axis=1)
-        fade_out[...] = jnp.broadcast_to(whole, (8, 128))
+        fade_out[...] = whole
 
     @pl.when(level == 0)
     def _():
@@ -872,8 +872,8 @@
                 pltpu.VMEM((rows, features), jnp.bfloat16),
                 pltpu.VMEM(state, jnp.bfloat16),
                 pltpu.VMEM(state, jnp.bfloat16),
-                pltpu.VMEM((8, 128), jnp.float32),
-                pltpu.VMEM((8, 128), jnp.float32),
+                pltpu.VMEM((1, 128), jnp.float32),
+                pltpu.VMEM((1, 128), jnp.float32),
                 pltpu.VMEM((links, 8, UNIT), jnp.float32),
                 pltpu.VMEM(state, jnp.float32),
                 pltpu.VMEM((links, 8, UNIT), jnp.float32),
@@ -881,9 +881,9 @@
             + [pltpu.VMEM(state, jnp.bfloat16)] * 5
             + [pltpu.VMEM(slab, jnp.bfloat16)] * 3
             + [
-                pltpu.VMEM((8, 128), jnp.int32),
-                pltpu.VMEM((devices, 8, 128), jnp.int32),
-                pltpu.SMEM((devices, 8, 128), jnp.int32),
+                pltpu.VMEM((1, 128), jnp.int32),
+                pltpu.VMEM((devices, 1, 128), jnp.int32),
+                pltpu.SMEM((devices, 1, 128), jnp.int32),
                 sems((2, PARTS)),
                 sems((2, links)),
                 sems((PARTS,)),

time: 114 us -> 113 us (level)
  no operation moved by 1% of the time
where the time goes in v6:
time: 113 us
  Pallas kernels  113 us (100%)
    pallas_call x1, Pallas kernels, local(): pl.pallas_call(functools.partial(fused_kernel, devices, PARTS), out_shape...  112 us

profile of v6, /device:TPU:16, one launch (start us, length us, event | category | flops | bytes accessed | tf_op | source)
XLA Modules:
  0.0 113.1 jit_solution(1988127674608752767)
XLA Ops:
  0.0 0.0 copy-start
  0.0 111.5 %fused.1 = (bf16[256,4096]{1,0:T(8,128)(2,1)S(1)}, f32[256,128]{1,0:T(8,128)S(1)}) custom-call(bf16[256,4096]{1,0:T(8,128)(2,1)} %x_hbm.1, bf16[256,4096]{1,0:T(8,128)(2,1)} %gate_hbm.1, bf16[64,256]{1,0:T(8,128)(2,1)} %bitcast.6, bf16[256,128]{1,0:T(8,128)(2,1)} %write_hbm.1, bf16[256,128]{1,0:T(8,128)(2,1)} %read_hbm.1, f32[1,64]{1,0:T(1,128)} %bitcast.7, ...), custom_call_target="tpu_custom_call" | custom-call | tf_op jit(solution)/shard_map/fused/pallas_call | solution.py:853
  111.5 0.0 copy-done
  111.5 1.6 %scale.1 = bf16[256,4096]{1,0:T(8,128)(2,1)} custom-call(bf16[256,4096]{1,0:T(8,128)(2,1)S(1)} %get-tuple-element.7.in_ref, f32[256,128]{1,0:T(8,128)S(1)} %get-tuple-element.8.squares_ref, f32[1,4096]{1,0:T(1,128)S(1)} %bitcast.5), custom_call_target="tpu_custom_call" | custom-call | tf_op jit(solution)/shard_map/scale/pallas_call | solution.py:921
Async XLA Ops:
  0.0 111.5 %copy-start = (f32[4096]{0:T(1024)S(1)}, f32[4096]{0:T(1024)}, u32[]{:S(2)}) copy-start(f32[4096]{0:T(1024)} %param.19) | copy-start | bytes 49156

commit v7 on v6

--- a/solution.py
+++ b/solution.py
@@ -429,6 +429,7 @@
 
     @pl.when(me == 0)
     def _():
+        near_entry[...] = jnp.zeros_like(near_entry)
         far_entry[...] = jnp.zeros_like(far_entry)
 
     def ends(c, carry):
@@ -534,6 +535,15 @@
             @pl.when(jnp.logical_and(j == s, jnp.logical_and(there != me, wanted)))
             def _():
                 first(there, s).start()
+
+    bottom = jnp.logical_and(level == 0, levels > 2)
+
+    def open_early():
+        load(1, 0).wait()
+        compute(0, side, near_entry)
+        hear_above()
+        for k in range(per):
+            outward(0, 2 * k + side, k >= levels // 2)
 
     late = parts - 1
     for j in range(late):
@@ -556,6 +566,16 @@
                 order_all[me] = held
                 scatter(dt, cums, cum_s, dt_s, range(2, chunks))
                 score_setup(dt, cums, read_ref, gain_ref, cum_s, write_t, *scratch[3:])
+
+            @pl.when(jnp.logical_and(below, level < levels - 2))
+            def _():
+                hear_above()
+                tell(ready_sem, me - 2)
+
+            @pl.when(jnp.logical_and(bottom, me == 0))
+            def _():
+                open_early()
+
         if j == 1:
             keep_half(0)
             keep_half(1)
@@ -569,24 +589,13 @@
             for u in range(units):
                 fade_s[c // 2 * units + u] = jnp.broadcast_to(lanes[:, u * UNIT : (u + 1) * UNIT], (8, UNIT))
 
-    @pl.when(jnp.logical_and(below, level < levels - 2))
-    def _():
-        hear_above()
-        tell(ready_sem, me - 2)
-
     @pl.when(low)
     def _():
         links(0)
 
-    bottom = jnp.logical_and(level == 0, levels > 2)
-
-    @pl.when(bottom)
+    @pl.when(jnp.logical_and(bottom, me > 0))
     def _():
-        hear_above()
-        load(1, 0).wait()
-        compute(0, side, near_entry)
-        for k in range(per):
-            outward(0, 2 * k + side, k >= levels // 2)
+        open_early()
 
     load(0, late).wait()
     swap_half(late)

time: 113 us -> 113 us (level)
  no operation moved by 1% of the time
where the time goes in v7:
time: 113 us
  Pallas kernels  113 us (100%)
    pallas_call x1, Pallas kernels, local(): pl.pallas_call(functools.partial(fused_kernel, devices, PARTS), out_shape...  111 us

profile of v7, /device:TPU:16, one launch (start us, length us, event | category | flops | bytes accessed | tf_op | source)
XLA Modules:
  0.0 112.9 jit_solution(8133611907542489524)
XLA Ops:
  0.0 0.0 copy-start
  0.0 111.4 %fused.1 = (bf16[256,4096]{1,0:T(8,128)(2,1)S(1)}, f32[256,128]{1,0:T(8,128)S(1)}) custom-call(bf16[256,4096]{1,0:T(8,128)(2,1)} %x_hbm.1, bf16[256,4096]{1,0:T(8,128)(2,1)} %gate_hbm.1, bf16[64,256]{1,0:T(8,128)(2,1)} %bitcast.6, bf16[256,128]{1,0:T(8,128)(2,1)} %write_hbm.1, bf16[256,128]{1,0:T(8,128)(2,1)} %read_hbm.1, f32[1,64]{1,0:T(1,128)} %bitcast.7, ...), custom_call_target="tpu_custom_call" | custom-call | tf_op jit(solution)/shard_map/fused/pallas_call | solution.py:862
  111.4 0.0 copy-done
  111.4 1.6 %scale.1 = bf16[256,4096]{1,0:T(8,128)(2,1)} custom-call(bf16[256,4096]{1,0:T(8,128)(2,1)S(1)} %get-tuple-element.7.in_ref, f32[256,128]{1,0:T(8,128)S(1)} %get-tuple-element.8.squares_ref, f32[1,4096]{1,0:T(1,128)S(1)} %bitcast.5), custom_call_target="tpu_custom_call" | custom-call | tf_op jit(solution)/shard_map/scale/pallas_call | solution.py:930
Async XLA Ops:
  0.0 111.4 %copy-start = (f32[4096]{0:T(1024)S(1)}, f32[4096]{0:T(1024)}, u32[]{:S(2)}) copy-start(f32[4096]{0:T(1024)} %param.19) | copy-start | bytes 49156

commit v8 on v7

--- a/solution.py
+++ b/solution.py
@@ -337,10 +337,9 @@
     def left(ref, sem):
         send(ref, ref, sem, sem, buddy).wait_send()
 
-    def load(which, j):
+    def load(j):
         cols = pl.ds(j * span, span)
-        source, target = ((x_hbm, x_ref), (gate_hbm, gate_ref))[which]
-        return pltpu.make_async_copy(source.at[:, cols], target.at[:, cols], load_sem.at[which, j])
+        return pltpu.make_async_copy(x_hbm.at[:, cols], x_ref.at[:, cols], load_sem.at[j])
 
     def pair(r):
         return send(pair_out.at[r], pair_in.at[r], link_send.at[0], link_recv.at[0, r], buddy)
@@ -397,15 +396,15 @@
     ]
     for copy in small[:5]:
         copy.start()
-    load(0, 0).start()
+    load(0).start()
     for copy in small[5:]:
         copy.start()
     for copy in small[:4]:
         copy.wait()
     for j in range(1, parts):
-        load(0, j).start()
-    for j in range(parts):
-        load(1, j).start()
+        load(j).start()
+    gate_load = pltpu.make_async_copy(gate_hbm, gate_ref, load_sem.at[parts])
+    gate_load.start()
 
     def send_orders():
         for off in range(1, n):
@@ -513,13 +512,6 @@
     def by_distance(k):
         return jnp.where(low, levels - 1 - k, k)
 
-    def gate_ready(j):
-        for s in range(parts):
-
-            @pl.when(j == s)
-            def _():
-                load(1, s).wait()
-
     def compute(j, i, entry):
         def put(g, value):
             for p in range(per):
@@ -539,7 +531,7 @@
     bottom = jnp.logical_and(level == 0, levels > 2)
 
     def open_early():
-        load(1, 0).wait()
+        gate_load.wait()
         compute(0, side, near_entry)
         hear_above()
         for k in range(per):
@@ -547,7 +539,7 @@
 
     late = parts - 1
     for j in range(late):
-        load(0, j).wait()
+        load(j).wait()
         swap_half(j)
         if j == 0:
 
@@ -597,7 +589,7 @@
     def _():
         open_early()
 
-    load(0, late).wait()
+    load(late).wait()
     swap_half(late)
     for j in range(2, parts):
         keep_half(j)
@@ -619,7 +611,10 @@
 
         @pl.when(jnp.logical_not(begun))
         def _():
-            gate_ready(j)
+            @pl.when(j == 0)
+            def _():
+                gate_load.wait()
+
             compute(j, side, near_entry)
 
         for k in range(per):
@@ -893,7 +888,7 @@
                 pltpu.VMEM((1, 128), jnp.int32),
                 pltpu.VMEM((devices, 1, 128), jnp.int32),
                 pltpu.SMEM((devices, 1, 128), jnp.int32),
-                sems((2, PARTS)),
+                sems((PARTS + 1,)),
                 sems((2, links)),
                 sems((PARTS,)),
                 sems((3,)),

time: 113 us -> 113 us (level)
  no operation moved by 1% of the time
where the time goes in v8:
time: 113 us
  Pallas kernels  113 us (100%)
    pallas_call x1, Pallas kernels, local(): pl.pallas_call(functools.partial(fused_kernel, devices, PARTS), out_shape...  111 us

profile of v8, /device:TPU:16, one launch (start us, length us, event | category | flops | bytes accessed | tf_op | source)
XLA Modules:
  0.0 112.9 jit_solution(7386016305407492989)
XLA Ops:
  0.0 0.0 copy-start
  0.0 111.3 %fused.1 = (bf16[256,4096]{1,0:T(8,128)(2,1)S(1)}, f32[256,128]{1,0:T(8,128)S(1)}) custom-call(bf16[256,4096]{1,0:T(8,128)(2,1)} %x_hbm.1, bf16[256,4096]{1,0:T(8,128)(2,1)} %gate_hbm.1, bf16[64,256]{1,0:T(8,128)(2,1)} %bitcast.6, bf16[256,128]{1,0:T(8,128)(2,1)} %write_hbm.1, bf16[256,128]{1,0:T(8,128)(2,1)} %read_hbm.1, f32[1,64]{1,0:T(1,128)} %bitcast.7, ...), custom_call_target="tpu_custom_call" | custom-call | tf_op jit(solution)/shard_map/fused/pallas_call | solution.py:857
  111.3 0.0 copy-done
  111.4 1.6 %scale.1 = bf16[256,4096]{1,0:T(8,128)(2,1)} custom-call(bf16[256,4096]{1,0:T(8,128)(2,1)S(1)} %get-tuple-element.7.in_ref, f32[256,128]{1,0:T(8,128)S(1)} %get-tuple-element.8.squares_ref, f32[1,4096]{1,0:T(1,128)S(1)} %bitcast.5), custom_call_target="tpu_custom_call" | custom-call | tf_op jit(solution)/shard_map/scale/pallas_call | solution.py:925
Async XLA Ops:
  0.0 111.3 %copy-start = (f32[4096]{0:T(1024)S(1)}, f32[4096]{0:T(1024)}, u32[]{:S(2)}) copy-start(f32[4096]{0:T(1024)} %param.19) | copy-start | bytes 49156
